TPU v7x, 32 devices: a whole 2x2x4 slice. The times are simulated.
32 devices in a mesh: gx: 16 (over z, x, core), gy: 2 (over y).
Axes of the slice: x: 2, y: 2, z: 4, core: 2. Of those that a mesh axis runs over, the one named last changes fastest.
Arguments:
- voltage: float32 [256, 64, 128], P('gx', 'gy'), may hold values from -0.5 to 1.5
- potential: float32 [256, 64, 128], P('gx', 'gy'), may hold values from -6 to 6
- tissue: int32 [256, 64, 128], P('gx', 'gy'), may hold values 0 or 1
- gain: float32 [256, 64, 128], P('gx', 'gy'), may hold values from 0.25 to 1.75
- couplings: float32 [2, 9], replicated, may hold values from 0.05 to 0.5
- line_factor: float32 [256, 256], replicated, as said below
Outputs:
- new_voltage: float32 [256, 64, 128], P('gx', 'gy')
- new_potential: float32 [256, 64, 128], P('gx', 'gy')
Inputs may be any that keep to these rules, and one draw needn't show every extreme that they name: line_factor is lower triangular with positive diagonal entries.
All inputs are finite; a program needn't handle non-finite values. No bound on the sum of `tissue` on one device may be relied on, other than what follows from the above.
Results may differ from a plain program's by a relative error of at most 0.0003.
Values sent between devices are 32-bit elements; how exact they have to be, the bound alone decides.
No kernel may reach another device: no remote copies, remote signals or barrier semaphores. Data moves between devices by JAX's collectives and lax.ppermute only.
A program may use at most 64 MiB of HBM per device.

v0:
```python
import jax
import jax.numpy as jnp
from jax import lax
from jax.experimental import pallas as pl
from jax.experimental.pallas import tpu as pltpu
from jax.sharding import PartitionSpec as P


CHEB = 8
ITERS = 4
SUB = 8
ROWS = 4
TILES = 8

time_step = 2.0
ionic_rate = 0.5
onset_level = 0.2
gain_top = 3.0625
f32 = jnp.float32
VMEM = pl.BlockSpec(memory_space=pltpu.VMEM)
SMEM = pl.BlockSpec(memory_space=pltpu.SMEM)


def up_to(n, m):
    return -(-n // m) * m


class Plan:
    def __init__(self, local_shape, ngx, ngy):
        self.nz, self.ny, self.nx = local_shape
        self.ngx, self.ngy = ngx, ngy
        self.depth = ITERS
        self.hz = CHEB + 1
        self.hy = up_to(CHEB + 1 + ITERS, SUB)
        self.swap = ngy == 2
        self.hops = []
        left, hop = self.hz, 1
        while left > 0:
            self.hops.append((hop, min(self.nz, left)))
            left -= self.nz
            hop += 1
        self.pad = up_to(ITERS + 1, SUB)
        self.ywin = self.ny + self.hy * (1 if self.swap else 2)
        self.yrows = self.ywin + 2 * self.pad
        self.zrows = up_to(max(self.hz - d + up_to(self.nz + 2 * d, SUB) + 1 for d in range(self.hz)), SUB)
        self.zrows = max(self.zrows, up_to(self.nz + 2 * self.hz, SUB))
        self.NZ = self.nz * ngx
        self.cols = self.nx // ngx
        self.wid = 1
        while self.wid < self.cols + 2 * self.depth:
            self.wid *= 2
        self.hx = (self.wid - self.cols) // 2
        self.grp = self.nx // self.wid
        self.slabs = -(-(self.ny + 2 * self.depth) // self.grp)
        self.back_grp = self.nx // self.cols
        self.back = self.ny // self.back_grp


def here():
    return lax.axis_index("gx"), lax.axis_index("gy")


def prep_kernel(plan, volt, pot, tissue, gain, cond, *outs):
    idx = here()
    cond[...] = tissue[...].astype(f32) * gain[...]
    fields = (volt, pot, cond)
    if plan.swap:
        ys = [pl.multiple_of((1 - idx[1]) * (plan.ny - plan.hy), SUB)]
    else:
        ys = [plan.ny - plan.hy, 0]
    at = 0
    for y0 in ys:
        for f, ref in enumerate(fields):
            outs[at][f] = ref[:, pl.ds(y0, plan.hy), :]
        at += 1
    for _, n in plan.hops:
        for z0 in (plan.nz - n, 0):
            for f, ref in enumerate(fields):
                outs[at][f] = ref[pl.ds(z0, n)]
            at += 1
            for y0 in ys:
                for f, ref in enumerate(fields):
                    outs[at][f] = ref[pl.ds(z0, n), pl.ds(y0, plan.hy), :]
                at += 1


def combine(tile, coef, left, right, width):
    k = coef
    mid, zp, zm, yp, ym = tile(0, 0), tile(1, 0), tile(-1, 0), tile(0, 1), tile(0, -1)
    zpyp, zmym, zpym, zmyp = tile(1, 1), tile(-1, -1), tile(1, -1), tile(-1, 1)
    same = k[0] * (zp + zm) + k[1] * (yp + ym) + k[3] * (zpyp + zmym) + k[4] * (zpym + zmyp)
    face = k[2] * mid
    plus = face + k[5] * zp + k[6] * zm + k[7] * yp + k[8] * ym
    minus = face + k[5] * zm + k[6] * zp + k[7] * ym + k[8] * yp
    plus = pltpu.roll(plus, width - 1, 1)
    minus = pltpu.roll(minus, 1, 1)
    if left is not None:
        plus = jnp.where(right, 0.0, plus)
        minus = jnp.where(left, 0.0, minus)
    return same + plus + minus


def cheb_kernel(plan, coup, volt, pot, cond, *rest):
    p = plan
    idx = here()
    ny_halo = 1 if p.swap else 2
    n_in = ny_halo + len(p.hops) * 2 * (1 + ny_halo)
    halos = rest[:n_in]
    new_volt, send = rest[n_in : n_in + 2]
    C, G0, G1, E, PT, R, U, CS = rest[n_in + 2 :]
    nx = p.nx
    flat = lambda ref: ref.reshape(p.yrows * p.zrows, nx)
    if p.swap:
        ylocal = p.pad + idx[1] * p.hy
        yhalo = [p.pad + (1 - idx[1]) * p.ny]
    else:
        ylocal = p.pad + p.hy
        yhalo = [p.pad, p.pad + p.hy + p.ny]

    zero_rows = jnp.zeros((p.pad, p.zrows, nx), f32)
    for ref in (C, G0, G1, E, PT, R, U, CS):
        ref[pl.ds(0, p.pad)] = zero_rows
        ref[pl.ds(p.pad + p.ywin, p.pad)] = zero_rows

    fc, fg, fe, fp, fr = (flat(r) for r in (C, G0, E, PT, R))

    def place(getter, planes, zrow0, yrow0, ycount):
        def one(z, carry):
            for t in range(ycount // SUB):
                v, q, c = getter(z, t)
                start = (yrow0 + t * SUB) * p.zrows + zrow0 + z
                rows = pl.ds(start, SUB, stride=p.zrows)
                s = v + q
                mask = jnp.where(c > 0.0, 1.0, 0.0)
                fc[rows, :] = c
                fg[rows, :] = c * s
                fe[rows, :] = s
                fp[rows, :] = q
                fr[rows, :] = (-ionic_rate) * mask * v * (v - onset_level) * (v - 1.0)
            return carry

        lax.fori_loop(0, planes, one, 0)

    def local(z, t):
        ys = pl.ds(t * SUB, SUB)
        return volt[z, ys, :], pot[z, ys, :], cond[z, ys, :]

    def piece(ref):
        def get(z, t):
            ys = pl.ds(t * SUB, SUB)
            return ref[0, z, ys, :], ref[1, z, ys, :], ref[2, z, ys, :]

        return get

    place(local, p.nz, p.hz, ylocal, p.ny)
    at = 0
    for y0 in yhalo:
        place(piece(halos[at]), p.nz, p.hz, y0, p.hy)
        at += 1
    done = 0
    for _, n in p.hops:
        for z0 in (p.hz - done - n, p.hz + p.nz + done):
            place(piece(halos[at]), n, z0, ylocal, p.ny)
            at += 1
            for y0 in yhalo:
                place(piece(halos[at]), n, z0, y0, p.hy)
                at += 1
        done += n

    lane = lax.broadcasted_iota(jnp.int32, (SUB, nx), 1)
    left, right = lane == 0, lane == nx - 1
    ki = [coup[0, k] for k in range(9)]
    ke = [coup[1, k] for k in range(9)]

    total = ki[0]
    for k in ki[1:]:
        total = total + k
    top = 1.0 + time_step * 4.0 * gain_top * jnp.full((SUB, nx), total, f32)
    centre = (top + 1.0) / 2.0
    half = (top - 1.0) / 2.0
    ratio = centre / half
    weight = 1.0 / ratio
    inv_centre = 1.0 / centre

    def sweep(d, body):
        tiles = up_to(p.nz + 2 * d, SUB) // SUB
        over = p.hy - p.depth - d
        y0 = p.pad + (idx[1] * over if p.swap else over)
        count = p.ny + (d + p.depth) * (1 if p.swap else 2)

        def block(i, carry):
            stores = []
            for r in range(ROWS):
                for t in range(tiles):
                    stores += body(y0 + i * ROWS + r, p.hz - d + t * SUB)
            for ref, where, value in stores:
                ref[where] = value
            return carry

        lax.fori_loop(0, -(-count // ROWS), block, 0)

    def tile_of(ref, y, z):
        return lambda dz, dy: ref[y + dy, pl.ds(z + dz, SUB), :]

    def first(y, z):
        rows = pl.ds(z, SUB)
        c = C[y, rows, :]
        s = E[y, rows, :]
        cs = c * combine(tile_of(C, y, z), ki, left, right, nx)
        flow = cs * s - c * combine(tile_of(G0, y, z), ki, left, right, nx)
        r = R[y, rows, :] - time_step * flow
        u = r * inv_centre
        at = (y, rows)
        return [(CS, at, cs), (R, at, r), (U, at, u), (E, at, s + u), (G1, at, c * u)]

    sweep(CHEB, first)
    bufs = [G0, G1]
    for k in range(1, CHEB):
        gin, gout = bufs[k % 2], bufs[(k + 1) % 2]
        nxt = 1.0 / (2.0 * ratio - weight)
        keep, add = nxt * weight, 2.0 * nxt / half
        weight = nxt
        last = k == CHEB - 1

        def step(y, z, gin=gin, gout=gout, keep=keep, add=add, last=last):
            rows = pl.ds(z, SUB)
            c = C[y, rows, :]
            u = U[y, rows, :]
            flow = CS[y, rows, :] * u - c * combine(tile_of(gin, y, z), ki, left, right, nx)
            r = R[y, rows, :] - (u + time_step * flow)
            u = keep * u + add * r
            e = E[y, rows, :] + u
            at = (y, rows)
            if last:
                return [(E, at, e), (gout, at, c * e)]
            return [(E, at, e), (R, at, r), (U, at, u), (gout, at, c * u)]

        sweep(CHEB - k, step)

    gin = bufs[CHEB % 2]
    ke_sum = ke[0]
    for k in ke[1:]:
        ke_sum = ke_sum + k
    ke_sum = 2.0 * ke_sum

    def final(y, z):
        rows = pl.ds(z, SUB)
        c = C[y, rows, :]
        flow = CS[y, rows, :] * E[y, rows, :] - c * combine(tile_of(gin, y, z), ki, left, right, nx)
        outer = ke_sum * PT[y, rows, :] - combine(tile_of(PT, y, z), ke, left, right, nx)
        return [(R, (y, rows), -flow - outer)]

    sweep(0, final)

    def give(z, carry):
        for t in range(p.ny // SUB):
            start = (ylocal + t * SUB) * p.zrows + p.hz + z
            rows = pl.ds(start, SUB, stride=p.zrows)
            new_volt[z, pl.ds(t * SUB, SUB), :] = fe[rows, :] - fp[rows, :]
        return carry

    lax.fori_loop(0, p.nz, give, 0)

    first_row = ylocal - p.depth

    def pack(s, carry):
        for zt in range(p.nz // SUB):
            rows = pl.ds(p.hz + zt * SUB, SUB)
            src = [R[first_row + q * p.slabs + s, rows, :] for q in range(p.grp)]
            windows(p, src, send, pl.multiple_of(s * p.nz + zt * SUB, SUB))
        return carry

    lax.fori_loop(0, p.slabs, pack, 0)


def windows(p, src, send, row):
    group = lax.broadcasted_iota(jnp.int32, (SUB, p.nx), 1) // p.wid
    for j in range(p.ngx):
        acc = None
        for q in range(p.grp):
            amount = (p.wid * q - (p.cols * j - p.hx)) % p.nx
            part = pltpu.roll(src[q], amount, 1) if amount else src[q]
            acc = part if acc is None else jnp.where(group == q, part, acc)
        send[j, pl.ds(row, SUB), :] = acc


def cond_kernel(plan, cond, *rest):
    p = plan
    *sides, send = rest
    idx = here()
    flat = cond.reshape(p.nz * p.ny, p.nx)
    flats = [ref.reshape(3 * p.nz * p.hy, p.nx) for ref in sides]

    def row_of(y, zt):
        if 0 <= y < p.ny:
            return flat[pl.ds(zt * SUB * p.ny + y, SUB, stride=p.ny), :]
        low = y < 0
        at = p.hy + y if low else y - p.ny
        if at >= p.hy:
            return jnp.zeros((SUB, p.nx), f32)
        ref = flats[0] if low else flats[-1]
        val = ref[pl.ds((2 * p.nz + zt * SUB) * p.hy + at, SUB, stride=p.hy), :]
        if p.swap:
            val = jnp.where(idx[1] == (1 if low else 0), val, 0.0)
        return val

    for s in range(p.slabs):
        for zt in range(p.nz // SUB):
            src = [row_of(q * p.slabs + s - p.depth, zt) for q in range(p.grp)]
            windows(p, src, send, s * p.nz + zt * SUB)


def factor_kernel(line, line_t, parts, size):
    scale = 1.0 / jnp.max(jnp.abs(line[...]), keepdims=True)
    a = line_t[...] * scale
    b = line[...] * scale
    g = jnp.dot(a, b, precision=lax.Precision.HIGHEST, preferred_element_type=f32)
    high = g.astype(jnp.bfloat16)
    n = g.shape[0]
    parts[:, pl.ds(0, n)] = high
    parts[:, pl.ds(n, n)] = (g - high.astype(f32)).astype(jnp.bfloat16)
    parts[:, pl.ds(2 * n, n)] = high

    def norm(m):
        return jnp.sqrt(jnp.sum(jnp.sum(m * m, axis=0, keepdims=True), axis=1, keepdims=True))

    n = norm(g)
    est = n
    m = g / n
    for power in range(3):
        mb = m.astype(jnp.bfloat16)
        m = jnp.dot(mb, mb, preferred_element_type=f32)
        n = norm(m)
        m = m / n
        root = n
        for _ in range(power + 1):
            root = jnp.sqrt(root)
        est = est * root
    size[...] = jnp.broadcast_to(est, size.shape)


class Line:
    def __init__(self, p):
        idx = here()
        self.p = p
        self.lane = lax.broadcasted_iota(jnp.int32, (SUB, p.nx), 1)
        self.idx = idx
        x = p.cols * idx[0] - p.hx + self.lane % p.wid
        self.xin = (x >= 0) & (x < p.nx)
        self.xown = (self.lane % p.wid >= p.hx) & (self.lane % p.wid < p.hx + p.cols)

    def ywin(self, s):
        return (self.lane // self.p.wid) * self.p.slabs + s

    def inside(self, s):
        p = self.p
        y = p.ny * self.idx[1] - p.depth + self.ywin(s)
        return self.xin & (y >= 0) & (y < p.ny * p.ngy)

    def own(self, s):
        p = self.p
        return self.xown & (self.ywin(s) >= p.depth) & (self.ywin(s) < p.depth + p.ny)

    def edges(self, ref):
        p = self.p
        for s in range(p.slabs + 2):
            ref[s, pl.ds(0, SUB), :] = jnp.zeros((SUB, p.nx), f32)
            ref[s, pl.ds(SUB + p.NZ, SUB), :] = jnp.zeros((SUB, p.nx), f32)

    def wrap(self, ref):
        p = self.p
        rows = pl.ds(SUB, p.NZ)
        ref[0, rows, :] = pltpu.roll(ref[p.slabs, rows, :], p.wid, 1)
        ref[p.slabs + 1, rows, :] = pltpu.roll(ref[1, rows, :], p.nx - p.wid, 1)

    def spread(self, recv, put):
        p = self.p
        for s in range(p.slabs):
            keep = self.inside(s)
            for j in range(p.ngx):
                for zt in range(p.nz // SUB):
                    got = recv[j, pl.ds(s * p.nz + zt * SUB, SUB), :]
                    put(s, j * p.nz + zt * SUB, jnp.where(keep, got, 0.0))

    def tile_of(self, ref, s, z):
        return lambda dz, dy: ref[s + 1 + dy, pl.ds(SUB + z + dz, SUB), :]


def line_kernel(plan, coup, recv, C, CS, G):
    p = plan
    nx = p.nx
    geo = Line(p)
    ki = [coup[0, k] for k in range(9)]
    geo.edges(G)

    def put(s, z, val):
        C[s, pl.ds(z, SUB), :] = val
        G[s + 1, pl.ds(SUB + z, SUB), :] = val

    geo.spread(recv, put)
    geo.wrap(G)
    step = TILES * SUB
    for s in range(p.slabs):

        def weigh(t, carry, s=s):
            vals = []
            for k in range(TILES):
                z = pl.multiple_of(t * step, step) + k * SUB
                vals.append((z, C[s, pl.ds(z, SUB), :] * combine(geo.tile_of(G, s, z), ki, None, None, nx)))
            for z, v in vals:
                CS[s, pl.ds(z, SUB), :] = v
            return carry

        lax.fori_loop(0, p.NZ // step, weigh, 0)


def basis_kernel(plan, coup, recv, factor, size, C, CS, basis, sums, G, W, B0, B1, B2, R0, BB):
    p = plan
    nx, off = p.nx, SUB
    geo = Line(p)
    wrap, tile_of, inside, own = geo.wrap, geo.tile_of, geo.inside, geo.own
    ki = [coup[0, k] for k in range(9)]
    ke = [coup[1, k] for k in range(9)]
    ki_sum, ke_sum = ki[0], ke[0]
    for k in range(1, 9):
        ki_sum = ki_sum + ki[k]
        ke_sum = ke_sum + ke[k]
    lam = 2.0 * (ki_sum + ke_sum) * size[...]
    quarter = 4.0 / lam
    ke_twice = 2.0 * ke_sum
    step = TILES * SUB
    geo.edges(G)
    geo.edges(W)

    def put(s, z, val):
        B0[s, pl.ds(z, SUB), :] = val
        R0[s, pl.ds(z, SUB), :] = val

    geo.spread(recv, put)

    ring = [B0, B1, B2]
    out = jnp.zeros((1, nx), f32)

    def lane_put(out, acc, at):
        v = jnp.sum(jnp.sum(acc, axis=1, keepdims=True), axis=0, keepdims=True)
        return jnp.where(lax.broadcasted_iota(jnp.int32, (1, nx), 1) == at, v, out)

    zero = jnp.zeros((SUB, nx), f32)
    slot = p.depth
    for j in range(p.depth):
        cur = ring[j % 3]
        prev = ring[(j + 2) % 3]
        new = ring[(j + 1) % 3]
        for s in range(p.slabs):
            b = cur[s]
            high = b.astype(jnp.bfloat16)
            cols = pl.ds(s * nx, nx)
            BB[pl.ds(0, p.NZ), cols] = high
            BB[pl.ds(p.NZ, p.NZ), cols] = high
            BB[pl.ds(2 * p.NZ, p.NZ), cols] = (b - high.astype(f32)).astype(jnp.bfloat16)
        prod = jnp.dot(factor[...], BB[...], preferred_element_type=f32)
        for s in range(p.slabs):
            part = prod[:, s * nx : (s + 1) * nx]
            basis[j, s] = part
            W[s + 1, pl.ds(off, p.NZ), :] = part
            G[s + 1, pl.ds(off, p.NZ), :] = part * C[s]
        wrap(W)
        wrap(G)
        accs = [zero] * (j + 2)
        for s in range(p.slabs):
            keep = inside(s)

            def apply(t, carry, s=s, keep=keep, j=j, cur=cur, prev=prev, new=new):
                res = list(carry)
                stores = []
                for k in range(TILES):
                    z = pl.multiple_of(t * step, step) + k * SUB
                    rows = pl.ds(z, SUB)
                    w = W[s + 1, pl.ds(off + z, SUB), :]
                    inner = combine(tile_of(G, s, z), ki, None, None, nx)
                    outer = combine(tile_of(W, s, z), ke, None, None, nx)
                    e = (CS[s, rows, :] + ke_twice) * w - C[s, rows, :] * inner - outer
                    e = jnp.where(keep, e, 0.0)
                    if j < p.depth - 1:
                        b = cur[s, rows, :]
                        if j == 0:
                            stores.append((rows, 0.5 * quarter * e - b))
                        else:
                            stores.append((rows, quarter * e - 2.0 * b - prev[s, rows, :]))
                    for i in range(j):
                        res[i] = res[i] + basis[i, s, rows, :] * e
                    res[j] = res[j] + w * e
                    res[j + 1] = res[j + 1] + w * R0[s, rows, :]
                for rows, value in stores:
                    new[s, rows, :] = value
                return tuple(res)

            got = lax.fori_loop(0, p.NZ // step, apply, tuple([zero] * (j + 2)))
            mine = own(s)
            accs = [a + jnp.where(mine, g, 0.0) for a, g in zip(accs, got)]
        out = lane_put(out, accs[j + 1], j)
        for i in range(j + 1):
            out = lane_put(out, accs[i], slot)
            slot += 1
    sums[...] = jnp.broadcast_to(out, sums.shape)


def solve_kernel(plan, recv, basis, send):
    p = plan
    nx, n = p.nx, p.depth
    tot = jnp.sum(recv[...], axis=0, keepdims=True)

    def get(k):
        return jnp.broadcast_to(tot[:, k : k + 1], (SUB, nx))

    rhs = [get(j) for j in range(n)]
    A = [[None] * n for _ in range(n)]
    slot = n
    for j in range(n):
        for i in range(j + 1):
            A[i][j] = A[j][i] = get(slot)
            slot += 1
    diag = [A[i][i] for i in range(n)]
    inv = [None] * n
    for k in range(n):
        ok = A[k][k] > 1e-7 * diag[k]
        inv[k] = jnp.where(ok, 1.0 / jnp.where(ok, A[k][k], 1.0), 0.0)
        for i in range(k + 1, n):
            m = A[i][k] * inv[k]
            for l in range(k + 1, n):
                A[i][l] = A[i][l] - m * A[k][l]
            rhs[i] = rhs[i] - m * rhs[k]
    sol = [None] * n
    for k in reversed(range(n)):
        acc = rhs[k]
        for l in range(k + 1, n):
            acc = acc - A[k][l] * sol[l]
        sol[k] = acc * inv[k]

    lane = lax.broadcasted_iota(jnp.int32, (SUB, nx), 1)
    group = lane // p.cols
    per = p.nz // SUB

    def pack(t, carry):
        rows = pl.ds(pl.multiple_of(t * SUB, SUB), SUB)
        dst = t // per
        part = []
        for s in range(p.slabs):
            acc = sol[0] * basis[0, s, rows, :]
            for i in range(1, n):
                acc = acc + sol[i] * basis[i, s, rows, :]
            part.append(acc)
        for o in range(p.back):
            acc = None
            for q2 in range(p.back_grp):
                y = p.depth + o * p.back_grp + q2
                q, s = y // p.slabs, y % p.slabs
                amount = (p.cols * q2 - (p.wid * q + p.hx)) % nx
                piece = pltpu.roll(part[s], amount, 1) if amount else part[s]
                acc = piece if acc is None else jnp.where(group == q2, piece, acc)
            send[dst, pl.ds(pl.multiple_of(o * p.nz + (t % per) * SUB, SUB), SUB), :] = acc
        return carry

    lax.fori_loop(0, p.NZ // SUB, pack, 0, unroll=2)


def finish_kernel(plan, recv, pot, out):
    p = plan
    nx = p.nx
    lane = lax.broadcasted_iota(jnp.int32, (SUB, nx), 1)
    group = lane // p.cols
    fpot = pot.reshape(p.nz * p.ny, nx)
    fout = out.reshape(p.nz * p.ny, nx)
    for o in range(p.back):
        for zt in range(p.nz // SUB):
            src = [recv[j, pl.ds(o * p.nz + zt * SUB, SUB), :] for j in range(p.ngx)]
            for q2 in range(p.back_grp):
                acc = None
                for j in range(p.ngx):
                    amount = (p.cols * j - p.cols * q2) % nx
                    piece = pltpu.roll(src[j], amount, 1) if amount else src[j]
                    acc = piece if acc is None else jnp.where(group == j, piece, acc)
                rows = pl.ds(zt * SUB * p.ny + o * p.back_grp + q2, SUB, stride=p.ny)
                fout[rows, :] = fpot[rows, :] + acc


def bidomain_step(voltage, potential, tissue, gain, couplings, line_factor):
    ngx, ngy = lax.axis_size("gx"), lax.axis_size("gy")
    p = Plan(voltage.shape, ngx, ngy)
    nz, ny, nx = p.nz, p.ny, p.nx
    sds = jax.ShapeDtypeStruct

    def call(kernel, ins, outs, scratch=()):
        return pl.pallas_call(
            kernel,
            out_shape=outs,
            in_specs=ins,
            out_specs=[VMEM] * len(outs),
            scratch_shapes=list(scratch),
            compiler_params=pltpu.CompilerParams(vmem_limit_bytes=58 * 1024 * 1024),
        )

    ysends = [None] if p.swap else [1, -1]
    shapes, routes = [], []

    def pairs(dz, dy):
        res = []
        for a in range(ngx):
            for b in range(ngy):
                if dy is None:
                    tb = (b + 1) % 2
                else:
                    tb = b + dy
                if 0 <= a + dz < ngx and 0 <= tb < ngy:
                    res.append((a * ngy + b, (a + dz) * ngy + tb))
        return res

    for dy in ysends:
        shapes.append(sds((3, nz, p.hy, nx), f32))
        routes.append((0, dy))
    for hop, n in p.hops:
        for sign in (1, -1):
            shapes.append(sds((3, n, ny, nx), f32))
            routes.append((sign * hop, 0))
            for dy in ysends:
                shapes.append(sds((3, n, p.hy, nx), f32))
                routes.append((sign * hop, dy))

    cond, *pieces = call(
        lambda *a: prep_kernel(p, *a), [VMEM] * 4, [sds(voltage.shape, f32)] + shapes
    )(voltage, potential, tissue, gain)
    halos = []
    for x, r in zip(pieces, routes):
        halos.append(lax.ppermute(x, ("gx", "gy"), pairs(*r)))

    line = pltpu.VMEM((p.slabs, p.NZ, nx), f32)
    wide = pltpu.VMEM((p.slabs + 2, p.NZ + 2 * SUB, nx), f32)
    half = pltpu.VMEM((3 * p.NZ, p.slabs * nx), jnp.bfloat16)

    def swap_lines(x):
        return lax.all_to_all(x, "gx", split_axis=0, concat_axis=0, tiled=True)

    sides = halos[: len(ysends)]
    (send_c,) = call(
        lambda *a: cond_kernel(p, *a), [VMEM] * (1 + len(sides)), [sds((ngx, p.slabs * nz, nx), f32)]
    )(cond, *sides)
    recv_c = swap_lines(send_c)
    line_c, line_cs = call(
        lambda *a: line_kernel(p, *a), [SMEM, VMEM], [sds((p.slabs, p.NZ, nx), f32)] * 2, [wide]
    )(couplings, recv_c)

    n_line = line_factor.shape[0]
    parts, size = call(
        factor_kernel, [VMEM] * 2, [sds((n_line, 3 * n_line), jnp.bfloat16), sds((SUB, nx), f32)]
    )(line_factor, line_factor.T)

    ext = pltpu.VMEM((p.yrows, p.zrows, nx), f32)
    new_voltage, send = call(
        lambda *a: cheb_kernel(p, *a),
        [SMEM] + [VMEM] * (3 + len(halos)),
        [sds(voltage.shape, f32), sds((ngx, p.slabs * nz, nx), f32)],
        [ext] * 8,
    )(couplings, voltage, potential, cond, *halos)

    recv = swap_lines(send)
    basis, sums = call(
        lambda *a: basis_kernel(p, *a),
        [SMEM] + [VMEM] * 5,
        [sds((p.depth, p.slabs, p.NZ, nx), f32), sds((ngx * ngy, nx), f32)],
        [wide, wide, line, line, line, line, half],
    )(couplings, recv, parts, size, line_c, line_cs)

    shares = lax.all_to_all(
        sums.reshape(ngx * ngy, 1, nx), ("gx", "gy"), split_axis=0, concat_axis=0, tiled=True
    ).reshape(ngx * ngy, nx)

    (back,) = call(
        lambda *a: solve_kernel(p, *a), [VMEM] * 2, [sds((ngx, p.back * nz, nx), f32)]
    )(shares, basis)
    home = lax.all_to_all(back, "gx", split_axis=0, concat_axis=0, tiled=True)
    (new_potential,) = call(
        lambda *a: finish_kernel(p, *a), [VMEM] * 2, [sds(voltage.shape, f32)]
    )(home, potential)
    return new_voltage, new_potential


def solution(mesh):
    spec = P("gx", "gy", None)
    return jax.shard_map(
        bidomain_step,
        mesh=mesh,
        in_specs=(spec, spec, spec, spec, P(), P()),
        out_specs=(spec, spec),
        check_vma=False,
    )
```

profile of v0, /device:TPU:0, one launch (start us, length us, event | category | flops | bytes accessed | tf_op | source)
XLA Modules:
  0.0 141.9 jit_solution(17482190323111663002)
XLA Ops:
  0.6 2.5 %shard_map.77 = (f32[16,32,128]{2,1,0:T(8,128)}, f32[3,16,16,128]{3,2,1,0:T(8,128)}, f32[3,9,32,128]{3,2,1,0:T(8,128)}, f32[3,9,16,128]{3,2,1,0:T(8,128)}, f32[3...) custom-call(f32[16,32,128]{2,1,0:T(8,128)} %a_1_.4, f32[16,32,128]{2,1,0:T(8,128)} %a_1_.5, s32[16,32,128]{2,1,0:T(8,128)} %a_2_.2, ...), custom_call_target="tpu_custom_call" | custom-call | tf_op jit(solution)/shard_map/pallas_call | solution.py:629
  3.1 0.0 copy-start.9
  3.1 0.0 copy-start.8
  3.1 0.0 copy-start.11
  3.1 0.0 copy-start.10
  3.2 3.1 %collective-permute-start = (f32[3,16,16,128]{3,2,1,0:T(8,128)}, f32[3,16,16,128]{3,2,1,0:T(8,128)S(1)}, u32[]{:S(2)}, u32[]{:S(2)}) collective-permute-start(f32[3,16,16,128]{3,2,1,0:T(8,128)} %get-tuple-element.17), channel_id=1, source_target_pairs={{0,1},{1,0},{2,3},{3,2},{4,5},{5,4},{6,7},{7,6},{8,9},{9,8},{10,11... | collective-permute-start | bytes 1179656 | tf_op jit(solution)/shard_map/ppermute | solution.py:634
  6.2 9.3 %collective-permute-done.a_4_.a_1_ = f32[3,16,16,128]{3,2,1,0:T(8,128)S(1)} collective-permute-done((f32[3,16,16,128]{3,2,1,0:T(8,128)}, f32[3,16,16,128]{3,2,1,0:T(8,128)S(1)}, u32[]{:S(2)}, u32[]{:S(2)}) %collective-permute-start) | collective-permute-done | bytes 393248 | tf_op jit(solution)/shard_map/ppermute | solution.py:634
  15.5 0.0 copy-start.2
  15.5 0.7 copy-done.2
  16.3 3.4 %shard_map.80 = f32[16,80,128]{2,1,0:T(8,128)} custom-call(f32[16,32,128]{2,1,0:T(8,128)} %get-tuple-element.16.a_3_.a_0_, f32[3,16,16,128]{3,2,1,0:T(8,128)} %copy-done.2), custom_call_target="tpu_custom_call" | custom-call | tf_op jit(solution)/shard_map/pallas_call | solution.py:644
  19.7 0.0 copy-start.3
  19.7 6.3 %all-to-all-start.1 = ((f32[16,80,128]{2,1,0:T(8,128)}), f32[16,80,128]{2,1,0:T(8,128)S(1)}, u32[]{:S(2)}, u32[]{:S(2)}) async-start(f32[16,80,128]{2,1,0:T(8,128)} %shard_map.80), calls=%async_computation.1 | async-start | bytes 1310720 | tf_op jit(solution)/shard_map/all_to_all | solution.py:641
  25.9 0.0 copy-done.9
  25.9 2.3 %collective-permute-start.1 = (f32[3,9,32,128]{3,2,1,0:T(8,128)S(1)}, f32[3,9,32,128]{3,2,1,0:T(8,128)S(1)}, u32[]{:S(2)}, u32[]{:S(2)}) collective-permute-start(f32[3,9,32,128]{3,2,1,0:T(8,128)S(1)} %copy-done.9), channel_id=1, source_target_pairs={{0,2},{1,3},{2,4},{3,5},{4,6},{5,7},{6,8},{7,9},{8,10},{9,11},{10,... | collective-permute-start | bytes 1327112 | tf_op jit(solution)/shard_map/ppermute | solution.py:634
  28.3 0.0 copy-done.8
  28.3 1.3 collective-permute-start.3
  29.6 0.0 copy-done.11
  29.6 5.3 %collective-permute-start.2 = (f32[3,9,16,128]{3,2,1,0:T(8,128)S(1)}, f32[3,9,16,128]{3,2,1,0:T(8,128)S(1)}, u32[]{:S(2)}, u32[]{:S(2)}) collective-permute-start(f32[3,9,16,128]{3,2,1,0:T(8,128)S(1)} %copy-done.11), channel_id=1, source_target_pairs={{0,3},{1,2},{2,5},{3,4},{4,7},{5,6},{6,9},{7,8},{8,11},{9,10},{10,... | collective-permute-start | bytes 663560 | tf_op jit(solution)/shard_map/ppermute | solution.py:634
  34.9 0.0 copy-done.10
  34.9 1.3 collective-permute-start.4
  36.2 2.1 %collective-permute-done.2.a_6_ = f32[3,9,16,128]{3,2,1,0:T(8,128)S(1)} collective-permute-done((f32[3,9,16,128]{3,2,1,0:T(8,128)S(1)}, f32[3,9,16,128]{3,2,1,0:T(8,128)S(1)}, u32[]{:S(2)}, u32[]{:S(2)}) %collective-permute-start.2) | collective-permute-done | bytes 221216 | tf_op jit(solution)/shard_map/ppermute | solution.py:634
  38.3 3.8 %collective-permute-done.4.a_8_ = f32[3,9,16,128]{3,2,1,0:T(8,128)S(1)} collective-permute-done((f32[3,9,16,128]{3,2,1,0:T(8,128)S(1)}, f32[3,9,16,128]{3,2,1,0:T(8,128)S(1)}, u32[]{:S(2)}, u32[]{:S(2)}) %collective-permute-start.4) | collective-permute-done | bytes 221216 | tf_op jit(solution)/shard_map/ppermute | solution.py:634
  42.2 0.0 copy-start.7
  42.2 0.0 collective-permute-done.1.a_5_
  42.2 0.0 copy-start.4
  42.2 0.0 collective-permute-done.3.a_7_
  42.2 0.0 copy-done.6
  42.2 0.7 copy-done.7
  42.8 0.1 copy-done.4
  43.0 0.0 copy-start.5
  43.0 0.8 copy-done.5
  43.7 17.5 %shard_map.78 = (f32[16,32,128]{2,1,0:T(8,128)}, f32[16,80,128]{2,1,0:T(8,128)}) custom-call(f32[2,9]{1,0:T(2,128)} %a_0_.7, f32[16,32,128]{2,1,0:T(8,128)} %a_1_.4, f32[16,32,128]{2,1,0:T(8,128)} %a_1_.5, f32[16,32,128]{2,1,0:T(8,128)} %get-tuple-element.16.a_3_.a_0_, f32[3,16,16,128]{3,2,1,0:T(8,128)} %copy-done.2, f32[3,9,32,128]{3,2,1,0:T(8,128)} %copy-done.4, ...), custom_call_target="tpu_custom_call" | custom-call | tf_op jit(solution)/shard_map/pallas_call | solution.py:658
  61.3 0.0 all-to-all-done.1.a_1_
  61.3 0.0 copy-start
  61.3 14.4 %all-to-all-start = ((f32[16,80,128]{2,1,0:T(8,128)}), f32[16,80,128]{2,1,0:T(8,128)S(1)}, u32[]{:S(2)}, u32[]{:S(2)}) async-start(f32[16,80,128]{2,1,0:T(8,128)} %get-tuple-element.23), calls=%async_computation | async-start | bytes 1310720 | tf_op jit(solution)/shard_map/all_to_all | solution.py:641
  75.7 0.0 copy-done.3
  75.7 0.8 copy.9
  76.5 3.4 %shard_map.79 = (bf16[256,768]{1,0:T(8,128)(2,1)}, f32[8,128]{1,0:T(8,128)}) custom-call(f32[256,256]{1,0:T(8,128)} %line.1, f32[256,256]{1,0:T(8,128)} %bitcast.5), custom_call_target="tpu_custom_call" | custom-call | tf_op jit(solution)/shard_map/pallas_call | solution.py:653
  79.9 0.0 copy-done
  79.9 4.1 %shard_map.81 = (f32[5,256,128]{2,1,0:T(8,128)}, f32[5,256,128]{2,1,0:T(8,128)}) custom-call(f32[2,9]{1,0:T(2,128)} %a_0_.7, f32[16,80,128]{2,1,0:T(8,128)} %copy-done), custom_call_target="tpu_custom_call" | custom-call | tf_op jit(solution)/shard_map/pallas_call | solution.py:648
  84.1 8.2 %all-to-all-done.a_1_ = f32[16,80,128]{2,1,0:T(8,128)S(1)} async-done(((f32[16,80,128]{2,1,0:T(8,128)}), f32[16,80,128]{2,1,0:T(8,128)S(1)}, u32[]{:S(2)}, u32[]{:S(2)}) %all-to-all-start) | async-done | bytes 655392 | tf_op jit(solution)/shard_map/all_to_all | solution.py:641
  92.3 0.0 copy-start.1
  92.3 0.8 copy-done.1
  93.1 15.8 %shard_map.82 = (f32[4,5,256,128]{3,2,1,0:T(8,128)}, f32[32,128]{1,0:T(8,128)}) custom-call(f32[2,9]{1,0:T(2,128)} %a_0_.7, f32[16,80,128]{2,1,0:T(8,128)} %copy-done.1, bf16[256,768]{1,0:T(8,128)(2,1)} %get-tuple-element.24.a_2_, f32[8,128]{1,0:T(8,128)} %get-tuple-element.25.a_3_, f32[5,256,128]{2,1,0:T(8,128)} %get-tuple-element.26.a_4_, ...), custom_call_target="tpu_custom_call" | custom-call | tf_op jit(solution)/shard_map/pallas_call | solution.py:666
  108.9 11.2 %all_to_all.20 = f32[32,1,128]{2,1,0:T(1,128)} all-to-all(f32[32,1,128]{2,1,0:T(1,128)} %bitcast.7), channel_id=1, replica_groups=mesh['gx'=16,'gy'=2] {'gx','gy'}, dimensions={0} | all-to-all | bytes 32768 | tf_op jit(solution)/shard_map/all_to_all | solution.py:673
  120.0 4.9 %shard_map.83 = f32[16,32,128]{2,1,0:T(8,128)} custom-call(f32[32,128]{1,0:T(8,128)} %bitcast.6, f32[4,5,256,128]{3,2,1,0:T(8,128)} %get-tuple-element.29.a_1_), custom_call_target="tpu_custom_call" | custom-call | tf_op jit(solution)/shard_map/pallas_call | solution.py:677
  124.9 14.2 %all_to_all.21.a_0_ = f32[16,32,128]{2,1,0:T(8,128)} all-to-all(f32[16,32,128]{2,1,0:T(8,128)} %shard_map.83), channel_id=1, replica_groups=mesh['gx'=16,'gy'=2] {'gx'}, dimensions={0} | all-to-all | bytes 524288 | tf_op jit(solution)/shard_map/all_to_all | solution.py:680
  139.1 2.8 %shard_map.84 = f32[16,32,128]{2,1,0:T(8,128)} custom-call(f32[16,32,128]{2,1,0:T(8,128)} %all_to_all.21.a_0_, f32[16,32,128]{2,1,0:T(8,128)} %a_1_.5), custom_call_target="tpu_custom_call" | custom-call | tf_op jit(solution)/shard_map/pallas_call | solution.py:681
  (1 shorter events, 0.0 us)
Async XLA Ops:
  3.1 22.8 %copy-start.9 = (f32[3,9,32,128]{3,2,1,0:T(8,128)S(1)}, f32[3,9,32,128]{3,2,1,0:T(8,128)}, u32[]{:S(2)}) copy-start(f32[3,9,32,128]{3,2,1,0:T(8,128)} %get-tuple-element.18) | copy-start | bytes 1327108
  3.1 25.1 %copy-start.8 = (f32[3,9,32,128]{3,2,1,0:T(8,128)S(1)}, f32[3,9,32,128]{3,2,1,0:T(8,128)}, u32[]{:S(2)}) copy-start(f32[3,9,32,128]{3,2,1,0:T(8,128)} %get-tuple-element.20) | copy-start | bytes 1327108
  3.1 26.5 %copy-start.11 = (f32[3,9,16,128]{3,2,1,0:T(8,128)S(1)}, f32[3,9,16,128]{3,2,1,0:T(8,128)}, u32[]{:S(2)}) copy-start(f32[3,9,16,128]{3,2,1,0:T(8,128)} %get-tuple-element.19) | copy-start | bytes 663556
  3.1 31.7 %copy-start.10 = (f32[3,9,16,128]{3,2,1,0:T(8,128)S(1)}, f32[3,9,16,128]{3,2,1,0:T(8,128)}, u32[]{:S(2)}) copy-start(f32[3,9,16,128]{3,2,1,0:T(8,128)} %get-tuple-element.21) | copy-start | bytes 663556
  3.2 12.4 %collective-permute-start = (f32[3,16,16,128]{3,2,1,0:T(8,128)}, f32[3,16,16,128]{3,2,1,0:T(8,128)S(1)}, u32[]{:S(2)}, u32[]{:S(2)}) collective-permute-start(f32[3,16,16,128]{3,2,1,0:T(8,128)} %get-tuple-element.17), channel_id=1, source_target_pairs={{0,1},{1,0},{2,3},{3,2},{4,5},{5,4},{6,7},{7,6},{8,9},{9,8},{10,11... | collective-permute-start | bytes 1179656 | tf_op jit(solution)/shard_map/ppermute | solution.py:634
  15.5 0.7 copy-start.2
  19.7 56.0 %copy-start.3 = (f32[256,256]{1,0:T(8,128)S(1)}, f32[256,256]{1,0:T(8,128)}, u32[]{:S(2)}) copy-start(f32[256,256]{1,0:T(8,128)} %line.1) | copy-start | bytes 786436
  19.7 41.6 %all-to-all-start.1 = ((f32[16,80,128]{2,1,0:T(8,128)}), f32[16,80,128]{2,1,0:T(8,128)S(1)}, u32[]{:S(2)}, u32[]{:S(2)}) async-start(f32[16,80,128]{2,1,0:T(8,128)} %shard_map.80), calls=%async_computation.1 | async-start | bytes 1310720 | tf_op jit(solution)/shard_map/all_to_all | solution.py:641
  25.9 16.2 %collective-permute-start.1 = (f32[3,9,32,128]{3,2,1,0:T(8,128)S(1)}, f32[3,9,32,128]{3,2,1,0:T(8,128)S(1)}, u32[]{:S(2)}, u32[]{:S(2)}) collective-permute-start(f32[3,9,32,128]{3,2,1,0:T(8,128)S(1)} %copy-done.9), channel_id=1, source_target_pairs={{0,2},{1,3},{2,4},{3,5},{4,6},{5,7},{6,8},{7,9},{8,10},{9,11},{10,... | collective-permute-start | bytes 1327112 | tf_op jit(solution)/shard_map/ppermute | solution.py:634
  28.3 13.9 %collective-permute-start.3 = (f32[3,9,32,128]{3,2,1,0:T(8,128)S(1)}, f32[3,9,32,128]{3,2,1,0:T(8,128)S(1)}, u32[]{:S(2)}, u32[]{:S(2)}) collective-permute-start(f32[3,9,32,128]{3,2,1,0:T(8,128)S(1)} %copy-done.8), channel_id=1, source_target_pairs={{2,0},{3,1},{4,2},{5,3},{6,4},{7,5},{8,6},{9,7},{10,8},{11,9},{12,... | collective-permute-start | bytes 1327112 | tf_op jit(solution)/shard_map/ppermute | solution.py:634
  29.6 8.7 %collective-permute-start.2 = (f32[3,9,16,128]{3,2,1,0:T(8,128)S(1)}, f32[3,9,16,128]{3,2,1,0:T(8,128)S(1)}, u32[]{:S(2)}, u32[]{:S(2)}) collective-permute-start(f32[3,9,16,128]{3,2,1,0:T(8,128)S(1)} %copy-done.11), channel_id=1, source_target_pairs={{0,3},{1,2},{2,5},{3,4},{4,7},{5,6},{6,9},{7,8},{8,11},{9,10},{10,... | collective-permute-start | bytes 663560 | tf_op jit(solution)/shard_map/ppermute | solution.py:634
  34.9 7.3 %collective-permute-start.4 = (f32[3,9,16,128]{3,2,1,0:T(8,128)S(1)}, f32[3,9,16,128]{3,2,1,0:T(8,128)S(1)}, u32[]{:S(2)}, u32[]{:S(2)}) collective-permute-start(f32[3,9,16,128]{3,2,1,0:T(8,128)S(1)} %copy-done.10), channel_id=1, source_target_pairs={{2,1},{3,0},{4,3},{5,2},{6,5},{7,4},{8,7},{9,6},{10,9},{11,8},{12,... | collective-permute-start | bytes 663560 | tf_op jit(solution)/shard_map/ppermute | solution.py:634
  38.3 3.9 %copy-start.6 = (f32[3,9,16,128]{3,2,1,0:T(8,128)}, f32[3,9,16,128]{3,2,1,0:T(8,128)S(1)}, u32[]{:S(2)}) copy-start(f32[3,9,16,128]{3,2,1,0:T(8,128)S(1)} %collective-permute-done.2.a_6_) | copy-start | bytes 663556
  42.2 0.7 copy-start.7
  42.2 0.8 copy-start.4
  43.0 0.8 copy-start.5
  61.3 18.7 %copy-start = (f32[16,80,128]{2,1,0:T(8,128)}, f32[16,80,128]{2,1,0:T(8,128)S(1)}, u32[]{:S(2)}) copy-start(f32[16,80,128]{2,1,0:T(8,128)S(1)} %all-to-all-done.1.a_1_) | copy-start | bytes 1966084
  61.3 31.0 %all-to-all-start = ((f32[16,80,128]{2,1,0:T(8,128)}), f32[16,80,128]{2,1,0:T(8,128)S(1)}, u32[]{:S(2)}, u32[]{:S(2)}) async-start(f32[16,80,128]{2,1,0:T(8,128)} %get-tuple-element.23), calls=%async_computation | async-start | bytes 1310720 | tf_op jit(solution)/shard_map/all_to_all | solution.py:641
  92.3 0.8 copy-start.1
where the time goes:
time: 143 us; the launch traced here: 142 us
  Pallas kernels  54.4 us (38%)
  starting transfers between devices  33.9 us (24%)
  blocking collectives  25.4 us (18%)
  waiting for transfers between devices  23.5 us (16%)
  local copies, waits for them, and re-layouts  4.01 us (3%)
    all_to_all x2, starting transfers between devices, swap_lines(): return lax.all_to_all(x, 'gx', split_axis=0, concat_axis=0, tiled=True)  20.7 us
    pallas_call x1, Pallas kernels, bidomain_step(): call(lambda *a: cheb_kernel(p, *a), [SMEM] + [VMEM] * (3 + len(halos)), [...  17.5 us
    pallas_call x1, Pallas kernels, bidomain_step(): call(lambda *a: basis_kernel(p, *a), [SMEM] + [VMEM] * 5, [sds((p.depth,...  15.8 us
    ppermute x5, waiting for transfers between devices, bidomain_step(): halos.append(lax.ppermute(x, ('gx', 'gy'), pairs(*r)))  15.3 us
    all_to_all x1, blocking collectives, bidomain_step(): home = lax.all_to_all(back, 'gx', split_axis=0, concat_axis=0, tiled=True)  14.2 us
    ppermute x5, starting transfers between devices, bidomain_step(): halos.append(lax.ppermute(x, ('gx', 'gy'), pairs(*r)))  13.3 us
    all_to_all x1, blocking collectives, bidomain_step(): lax.all_to_all(sums.reshape(ngx * ngy, 1, nx), ('gx', 'gy'), split_axis=0...  11.2 us
    all_to_all x2, waiting for transfers between devices, swap_lines(): return lax.all_to_all(x, 'gx', split_axis=0, concat_axis=0, tiled=True)  8.2 us
  transfers between devices with their start and end apart: 7, of which 4 were waited for; matrix products, arithmetic and copies ran while one was open for 1% of the time, Pallas kernels for 18%

commit v1 on v0

--- a/solution.py
+++ b/solution.py
@@ -60,9 +60,22 @@
     return lax.axis_index("gx"), lax.axis_index("gy")
 
 
-def prep_kernel(plan, volt, pot, tissue, gain, cond, *outs):
+def prep_kernel(plan, volt_hbm, pot_hbm, tissue_hbm, gain_hbm, volt, pot, cond, *rest):
+    *outs, tissue, gain, sems = rest
     idx = here()
+    moves = [
+        pltpu.make_async_copy(src, dst, sems.at[i])
+        for i, (src, dst) in enumerate(
+            ((tissue_hbm, tissue), (gain_hbm, gain), (volt_hbm, volt), (pot_hbm, pot))
+        )
+    ]
+    for move in moves:
+        move.start()
+    moves[0].wait()
+    moves[1].wait()
     cond[...] = tissue[...].astype(f32) * gain[...]
+    moves[2].wait()
+    moves[3].wait()
     fields = (volt, pot, cond)
     if plan.swap:
         ys = [pl.multiple_of((1 - idx[1]) * (plan.ny - plan.hy), SUB)]
@@ -84,20 +97,24 @@
                 at += 1
 
 
-def combine(tile, coef, left, right, width):
-    k = coef
+def mixed(k):
+    k = list(k)
+    return k[:5] + [0.5 * (k[5] + k[6]), 0.5 * (k[5] - k[6]), 0.5 * (k[7] + k[8]), 0.5 * (k[7] - k[8])]
+
+
+def combine(tile, k, left, right, width):
     mid, zp, zm, yp, ym = tile(0, 0), tile(1, 0), tile(-1, 0), tile(0, 1), tile(0, -1)
     zpyp, zmym, zpym, zmyp = tile(1, 1), tile(-1, -1), tile(1, -1), tile(-1, 1)
-    same = k[0] * (zp + zm) + k[1] * (yp + ym) + k[3] * (zpyp + zmym) + k[4] * (zpym + zmyp)
-    face = k[2] * mid
-    plus = face + k[5] * zp + k[6] * zm + k[7] * yp + k[8] * ym
-    minus = face + k[5] * zm + k[6] * zp + k[7] * ym + k[8] * yp
-    plus = pltpu.roll(plus, width - 1, 1)
-    minus = pltpu.roll(minus, 1, 1)
+    zs, ys = zp + zm, yp + ym
+    same = (k[0] * zs + k[1] * ys) + (k[3] * (zpyp + zmym) + k[4] * (zpym + zmyp))
+    even = k[2] * mid + (k[5] * zs + k[7] * ys)
+    odd = k[6] * (zp - zm) + k[8] * (yp - ym)
+    plus = pltpu.roll(even + odd, width - 1, 1)
+    minus = pltpu.roll(even - odd, 1, 1)
     if left is not None:
         plus = jnp.where(right, 0.0, plus)
         minus = jnp.where(left, 0.0, minus)
-    return same + plus + minus
+    return same + (plus + minus)
 
 
 def cheb_kernel(plan, coup, volt, pot, cond, *rest):
@@ -107,7 +124,7 @@
     n_in = ny_halo + len(p.hops) * 2 * (1 + ny_halo)
     halos = rest[:n_in]
     new_volt, send = rest[n_in : n_in + 2]
-    C, G0, G1, E, PT, R, U, CS = rest[n_in + 2 :]
+    C, G0, G1, E, PT, R, U, D, C2 = rest[n_in + 2 :]
     nx = p.nx
     flat = lambda ref: ref.reshape(p.yrows * p.zrows, nx)
     if p.swap:
@@ -118,7 +135,7 @@
         yhalo = [p.pad, p.pad + p.hy + p.ny]
 
     zero_rows = jnp.zeros((p.pad, p.zrows, nx), f32)
-    for ref in (C, G0, G1, E, PT, R, U, CS):
+    for ref in (C, G0, G1, E, PT, R, U, D, C2):
         ref[pl.ds(0, p.pad)] = zero_rows
         ref[pl.ds(p.pad + p.ywin, p.pad)] = zero_rows
 
@@ -171,10 +188,12 @@
     left, right = lane == 0, lane == nx - 1
     ki = [coup[0, k] for k in range(9)]
     ke = [coup[1, k] for k in range(9)]
-
-    total = ki[0]
-    for k in ki[1:]:
-        total = total + k
+    total, ke_sum = ki[0], ke[0]
+    for k in range(1, 9):
+        total = total + ki[k]
+        ke_sum = ke_sum + ke[k]
+    ke_sum = 2.0 * ke_sum
+    ki, ke = mixed(ki), mixed(ke)
     top = 1.0 + time_step * 4.0 * gain_top * jnp.full((SUB, nx), total, f32)
     centre = (top + 1.0) / 2.0
     half = (top - 1.0) / 2.0
@@ -206,12 +225,12 @@
         rows = pl.ds(z, SUB)
         c = C[y, rows, :]
         s = E[y, rows, :]
-        cs = c * combine(tile_of(C, y, z), ki, left, right, nx)
-        flow = cs * s - c * combine(tile_of(G0, y, z), ki, left, right, nx)
-        r = R[y, rows, :] - time_step * flow
+        c2 = time_step * c
+        cs = c2 * combine(tile_of(C, y, z), ki, left, right, nx)
+        r = R[y, rows, :] - (cs * s - c2 * combine(tile_of(G0, y, z), ki, left, right, nx))
         u = r * inv_centre
         at = (y, rows)
-        return [(CS, at, cs), (R, at, r), (U, at, u), (E, at, s + u), (G1, at, c * u)]
+        return [(D, at, 1.0 + cs), (C2, at, c2), (R, at, r), (U, at, u), (E, at, s + u), (G1, at, c * u)]
 
     sweep(CHEB, first)
     bufs = [G0, G1]
@@ -226,8 +245,8 @@
             rows = pl.ds(z, SUB)
             c = C[y, rows, :]
             u = U[y, rows, :]
-            flow = CS[y, rows, :] * u - c * combine(tile_of(gin, y, z), ki, left, right, nx)
-            r = R[y, rows, :] - (u + time_step * flow)
+            flow = D[y, rows, :] * u - C2[y, rows, :] * combine(tile_of(gin, y, z), ki, left, right, nx)
+            r = R[y, rows, :] - flow
             u = keep * u + add * r
             e = E[y, rows, :] + u
             at = (y, rows)
@@ -238,17 +257,13 @@
         sweep(CHEB - k, step)
 
     gin = bufs[CHEB % 2]
-    ke_sum = ke[0]
-    for k in ke[1:]:
-        ke_sum = ke_sum + k
-    ke_sum = 2.0 * ke_sum
 
     def final(y, z):
         rows = pl.ds(z, SUB)
-        c = C[y, rows, :]
-        flow = CS[y, rows, :] * E[y, rows, :] - c * combine(tile_of(gin, y, z), ki, left, right, nx)
+        e = E[y, rows, :]
+        flow = (D[y, rows, :] - 1.0) * e - C2[y, rows, :] * combine(tile_of(gin, y, z), ki, left, right, nx)
         outer = ke_sum * PT[y, rows, :] - combine(tile_of(PT, y, z), ke, left, right, nx)
-        return [(R, (y, rows), -flow - outer)]
+        return [(R, (y, rows), (-1.0 / time_step) * flow - outer)]
 
     sweep(0, final)
 
@@ -390,7 +405,11 @@
     p = plan
     nx = p.nx
     geo = Line(p)
-    ki = [coup[0, k] for k in range(9)]
+    ki = mixed([coup[0, k] for k in range(9)])
+    ke_sum = coup[1, 0]
+    for k in range(1, 9):
+        ke_sum = ke_sum + coup[1, k]
+    ke_twice = 2.0 * ke_sum
     geo.edges(G)
 
     def put(s, z, val):
@@ -406,7 +425,8 @@
             vals = []
             for k in range(TILES):
                 z = pl.multiple_of(t * step, step) + k * SUB
-                vals.append((z, C[s, pl.ds(z, SUB), :] * combine(geo.tile_of(G, s, z), ki, None, None, nx)))
+                part = combine(geo.tile_of(G, s, z), ki, None, None, nx)
+                vals.append((z, ke_twice + C[s, pl.ds(z, SUB), :] * part))
             for z, v in vals:
                 CS[s, pl.ds(z, SUB), :] = v
             return carry
@@ -427,7 +447,7 @@
         ke_sum = ke_sum + ke[k]
     lam = 2.0 * (ki_sum + ke_sum) * size[...]
     quarter = 4.0 / lam
-    ke_twice = 2.0 * ke_sum
+    ki, ke = mixed(ki), mixed(ke)
     step = TILES * SUB
     geo.edges(G)
     geo.edges(W)
@@ -479,7 +499,7 @@
                     w = W[s + 1, pl.ds(off + z, SUB), :]
                     inner = combine(tile_of(G, s, z), ki, None, None, nx)
                     outer = combine(tile_of(W, s, z), ke, None, None, nx)
-                    e = (CS[s, rows, :] + ke_twice) * w - C[s, rows, :] * inner - outer
+                    e = CS[s, rows, :] * w - C[s, rows, :] * inner - outer
                     e = jnp.where(keep, e, 0.0)
                     if j < p.depth - 1:
                         b = cur[s, rows, :]
@@ -590,14 +610,14 @@
     nz, ny, nx = p.nz, p.ny, p.nx
     sds = jax.ShapeDtypeStruct
 
-    def call(kernel, ins, outs, scratch=()):
+    def call(kernel, ins, outs, scratch=(), mib=12):
         return pl.pallas_call(
             kernel,
             out_shape=outs,
             in_specs=ins,
             out_specs=[VMEM] * len(outs),
             scratch_shapes=list(scratch),
-            compiler_params=pltpu.CompilerParams(vmem_limit_bytes=58 * 1024 * 1024),
+            compiler_params=pltpu.CompilerParams(vmem_limit_bytes=mib * 1024 * 1024),
         )
 
     ysends = [None] if p.swap else [1, -1]
@@ -626,9 +646,12 @@
                 shapes.append(sds((3, n, p.hy, nx), f32))
                 routes.append((sign * hop, dy))
 
-    cond, *pieces = call(
-        lambda *a: prep_kernel(p, *a), [VMEM] * 4, [sds(voltage.shape, f32)] + shapes
-    )(voltage, potential, tissue, gain)
+    volt, pot, cond, *pieces = call(
+        lambda *a: prep_kernel(p, *a),
+        [pl.BlockSpec(memory_space=pltpu.HBM)] * 4,
+        [sds(voltage.shape, f32)] * 3 + shapes,
+        [pltpu.VMEM(voltage.shape, jnp.int32), pltpu.VMEM(voltage.shape, f32), pltpu.SemaphoreType.DMA((4,))],
+    )(*(pltpu.with_memory_space_constraint(x, pltpu.HBM) for x in (voltage, potential, tissue, gain)))
     halos = []
     for x, r in zip(pieces, routes):
         halos.append(lax.ppermute(x, ("gx", "gy"), pairs(*r)))
@@ -659,8 +682,9 @@
         lambda *a: cheb_kernel(p, *a),
         [SMEM] + [VMEM] * (3 + len(halos)),
         [sds(voltage.shape, f32), sds((ngx, p.slabs * nz, nx), f32)],
-        [ext] * 8,
-    )(couplings, voltage, potential, cond, *halos)
+        [ext] * 9,
+        mib=24,
+    )(couplings, volt, pot, cond, *halos)
 
     recv = swap_lines(send)
     basis, sums = call(
@@ -668,6 +692,7 @@
         [SMEM] + [VMEM] * 5,
         [sds((p.depth, p.slabs, p.NZ, nx), f32), sds((ngx * ngy, nx), f32)],
         [wide, wide, line, line, line, line, half],
+        mib=24,
     )(couplings, recv, parts, size, line_c, line_cs)
 
     shares = lax.all_to_all(
@@ -680,7 +705,7 @@
     home = lax.all_to_all(back, "gx", split_axis=0, concat_axis=0, tiled=True)
     (new_potential,) = call(
         lambda *a: finish_kernel(p, *a), [VMEM] * 2, [sds(voltage.shape, f32)]
-    )(home, potential)
+    )(home, pot)
     return new_voltage, new_potential
 
 

time: 143 us -> 127 us (0.89)
  Pallas kernels: 54.4 us -> 41.3 us
  local copies, waits for them, and re-layouts: 4.01 us -> 0.14 us
  waiting for transfers between devices: 23.5 us -> 27.1 us
  blocking collectives: 25.4 us -> 23.3 us
    unnamed x25 -> x5, local copies, waits for them, and re-layouts: 4.01 us -> 0.14 us
    all_to_all x2, waiting for transfers between devices: 8.2 us -> 12 us  [swap_lines(): return lax.all_to_all(x, 'gx', split_axis=0, concat_axis=0, tiled=True)]
    pallas_call x1, Pallas kernels: 15.8 us -> 13.3 us  [bidomain_step(): call(lambda *a: basis_kernel(p, *a), [SMEM] + [VMEM] * 5, [sds((p.depth,...]
    pallas_call x1, Pallas kernels: 4.9 us -> 2.43 us  [bidomain_step(): call(lambda *a: solve_kernel(p, *a), [VMEM] * 2, [sds((ngx, p.back * nz,...]
    pallas_call x1, Pallas kernels: 17.5 us -> 15.8 us  [bidomain_step(): call(lambda *a: cheb_kernel(p, *a), [SMEM] + [VMEM] * (3 + len(halos)), [...]
    pallas_call x1, Pallas kernels: 3.38 us -> 1.74 us  [bidomain_step(): call(factor_kernel, [VMEM] * 2, [sds((n_line, 3 * n_line), jnp.bfloat16),...]
    all_to_all x1, blocking collectives: 14.2 us -> 12.6 us  [bidomain_step(): home = lax.all_to_all(back, 'gx', split_axis=0, concat_axis=0, tiled=True)]
    pallas_call x1, Pallas kernels: 4.14 us -> 2.63 us  [bidomain_step(): call(lambda *a: line_kernel(p, *a), [SMEM, VMEM], [sds((p.slabs, p.NZ, nx...]
  transfers between devices with their start and end apart: 7 -> 7, of which waited for: 4 -> 4; matrix products, arithmetic and copies ran while one was open for 1% -> 0% of each run, Pallas kernels for 18% -> 16%
where the time goes in v1:
time: 127 us
  Pallas kernels  41.3 us (33%)
  starting transfers between devices  34 us (27%)
  waiting for transfers between devices  27.1 us (21%)
  blocking collectives  23.3 us (18%)
    all_to_all x2, starting transfers between devices, swap_lines(): return lax.all_to_all(x, 'gx', split_axis=0, concat_axis=0, tiled=True)  20.7 us
    pallas_call x1, Pallas kernels, bidomain_step(): call(lambda *a: cheb_kernel(p, *a), [SMEM] + [VMEM] * (3 + len(halos)), [...  15.8 us
    ppermute x5, waiting for transfers between devices, bidomain_step(): halos.append(lax.ppermute(x, ('gx', 'gy'), pairs(*r)))  15.1 us
    ppermute x5, starting transfers between devices, bidomain_step(): halos.append(lax.ppermute(x, ('gx', 'gy'), pairs(*r)))  13.3 us
    pallas_call x1, Pallas kernels, bidomain_step(): call(lambda *a: basis_kernel(p, *a), [SMEM] + [VMEM] * 5, [sds((p.depth,...  13.3 us
    all_to_all x1, blocking collectives, bidomain_step(): home = lax.all_to_all(back, 'gx', split_axis=0, concat_axis=0, tiled=True)  12.6 us
    all_to_all x2, waiting for transfers between devices, swap_lines(): return lax.all_to_all(x, 'gx', split_axis=0, concat_axis=0, tiled=True)  12 us
    all_to_all x1, blocking collectives, bidomain_step(): lax.all_to_all(sums.reshape(ngx * ngy, 1, nx), ('gx', 'gy'), split_axis=0...  10.7 us
  transfers between devices with their start and end apart: 7, of which 4 were waited for; matrix products, arithmetic and copies ran while one was open for 0% of the time, Pallas kernels for 16%

profile of v1, /device:TPU:0, one launch (start us, length us, event | category | flops | bytes accessed | tf_op | source)
XLA Modules:
  0.0 126.6 jit_solution(4560572000444147737)
XLA Ops:
  0.6 0.0 copy-start.1
  0.6 1.3 %shard_map.77 = (f32[16,32,128]{2,1,0:T(8,128)S(1)}, f32[16,32,128]{2,1,0:T(8,128)S(1)}, f32[16,32,128]{2,1,0:T(8,128)S(1)}, f32[3,16,16,128]{3,2,1,0:T(8,128)S(...) custom-call(f32[16,32,128]{2,1,0:T(8,128)} %a_0_.4, ...), custom_call_target="tpu_custom_call" | custom-call | tf_op jit(solution)/shard_map/pallas_call | solution.py:649
  2.0 3.1 %collective-permute-start = (f32[3,16,16,128]{3,2,1,0:T(8,128)S(1)}, f32[3,16,16,128]{3,2,1,0:T(8,128)S(1)}, u32[]{:S(2)}, u32[]{:S(2)}) collective-permute-start(f32[3,16,16,128]{3,2,1,0:T(8,128)S(1)} %get-tuple-element.21), channel_id=1, source_target_pairs={{0,1},{1,0},{2,3},{3,2},{4,5},{5,4},{6,7},{7,6},{8,9},{9,8},{10,11... | collective-permute-start | bytes 1179656 | tf_op jit(solution)/shard_map/ppermute | solution.py:657
  5.0 9.1 %collective-permute-done.a_4_.a_1_ = f32[3,16,16,128]{3,2,1,0:T(8,128)S(1)} collective-permute-done((f32[3,16,16,128]{3,2,1,0:T(8,128)S(1)}, f32[3,16,16,128]{3,2,1,0:T(8,128)S(1)}, u32[]{:S(2)}, u32[]{:S(2)}) %collective-permute-start) | collective-permute-done | bytes 393248 | tf_op jit(solution)/shard_map/ppermute | solution.py:657
  14.2 2.3 %shard_map.80 = f32[16,80,128]{2,1,0:T(8,128)} custom-call(f32[16,32,128]{2,1,0:T(8,128)S(1)} %get-tuple-element.20.a_3_.a_0_, f32[3,16,16,128]{3,2,1,0:T(8,128)S(1)} %collective-permute-done.a_4_.a_1_), custom_call_target="tpu_custom_call" | custom-call | tf_op jit(solution)/shard_map/pallas_call | solution.py:667
  16.5 0.0 copy-start
  16.5 6.3 %all-to-all-start.1 = ((f32[16,80,128]{2,1,0:T(8,128)}), f32[16,80,128]{2,1,0:T(8,128)S(1)}, u32[]{:S(2)}, u32[]{:S(2)}) async-start(f32[16,80,128]{2,1,0:T(8,128)} %shard_map.80), calls=%async_computation.1 | async-start | bytes 1310720 | tf_op jit(solution)/shard_map/all_to_all | solution.py:664
  22.7 2.3 %collective-permute-start.1 = (f32[3,9,32,128]{3,2,1,0:T(8,128)S(1)}, f32[3,9,32,128]{3,2,1,0:T(8,128)S(1)}, u32[]{:S(2)}, u32[]{:S(2)}) collective-permute-start(f32[3,9,32,128]{3,2,1,0:T(8,128)S(1)} %get-tuple-element.22), channel_id=1, source_target_pairs={{0,2},{1,3},{2,4},{3,5},{4,6},{5,7},{6,8},{7,9},{8,10},{9,11},{10,... | collective-permute-start | bytes 1327112 | tf_op jit(solution)/shard_map/ppermute | solution.py:657
  25.1 1.3 %collective-permute-start.3 = (f32[3,9,32,128]{3,2,1,0:T(8,128)S(1)}, f32[3,9,32,128]{3,2,1,0:T(8,128)S(1)}, u32[]{:S(2)}, u32[]{:S(2)}) collective-permute-start(f32[3,9,32,128]{3,2,1,0:T(8,128)S(1)} %get-tuple-element.24), channel_id=1, source_target_pairs={{2,0},{3,1},{4,2},{5,3},{6,4},{7,5},{8,6},{9,7},{10,8},{11,9},{12,... | collective-permute-start | bytes 1327112 | tf_op jit(solution)/shard_map/ppermute | solution.py:657
  26.4 5.3 %collective-permute-start.2 = (f32[3,9,16,128]{3,2,1,0:T(8,128)S(1)}, f32[3,9,16,128]{3,2,1,0:T(8,128)S(1)}, u32[]{:S(2)}, u32[]{:S(2)}) collective-permute-start(f32[3,9,16,128]{3,2,1,0:T(8,128)S(1)} %get-tuple-element.23), channel_id=1, source_target_pairs={{0,3},{1,2},{2,5},{3,4},{4,7},{5,6},{6,9},{7,8},{8,11},{9,10},{10,... | collective-permute-start | bytes 663560 | tf_op jit(solution)/shard_map/ppermute | solution.py:657
  31.7 1.3 %collective-permute-start.4 = (f32[3,9,16,128]{3,2,1,0:T(8,128)S(1)}, f32[3,9,16,128]{3,2,1,0:T(8,128)S(1)}, u32[]{:S(2)}, u32[]{:S(2)}) collective-permute-start(f32[3,9,16,128]{3,2,1,0:T(8,128)S(1)} %get-tuple-element.25), channel_id=1, source_target_pairs={{2,1},{3,0},{4,3},{5,2},{6,5},{7,4},{8,7},{9,6},{10,9},{11,8},{12,... | collective-permute-start | bytes 663560 | tf_op jit(solution)/shard_map/ppermute | solution.py:657
  33.0 2.1 %collective-permute-done.2.a_6_ = f32[3,9,16,128]{3,2,1,0:T(8,128)S(1)} collective-permute-done((f32[3,9,16,128]{3,2,1,0:T(8,128)S(1)}, f32[3,9,16,128]{3,2,1,0:T(8,128)S(1)}, u32[]{:S(2)}, u32[]{:S(2)}) %collective-permute-start.2) | collective-permute-done | bytes 221216 | tf_op jit(solution)/shard_map/ppermute | solution.py:657
  35.1 3.8 %collective-permute-done.4.a_8_ = f32[3,9,16,128]{3,2,1,0:T(8,128)S(1)} collective-permute-done((f32[3,9,16,128]{3,2,1,0:T(8,128)S(1)}, f32[3,9,16,128]{3,2,1,0:T(8,128)S(1)}, u32[]{:S(2)}, u32[]{:S(2)}) %collective-permute-start.4) | collective-permute-done | bytes 221216 | tf_op jit(solution)/shard_map/ppermute | solution.py:657
  38.9 0.0 collective-permute-done.1.a_5_
  38.9 0.0 collective-permute-done.3.a_7_
  38.9 0.0 copy-done.1
  38.9 15.8 %shard_map.78 = (f32[16,32,128]{2,1,0:T(8,128)}, f32[16,80,128]{2,1,0:T(8,128)}) custom-call(f32[2,9]{1,0:T(2,128)S(1)} %copy-done.1, f32[16,32,128]{2,1,0:T(8,128)S(1)} %get-tuple-element.18.a_1_, f32[16,32,128]{2,1,0:T(8,128)S(1)} %get-tuple-element.19.a_2_.a_1_, f32[16,32,128]{2,1,0:T(8,128)S(1)} %get-tuple-element.20.a_3_.a_0_, ...), custom_call_target="tpu_custom_call" | custom-call | tf_op jit(solution)/shard_map/pallas_call | solution.py:681
  54.7 0.0 all-to-all-done.1.a_1_
  54.7 14.5 %all-to-all-start = ((f32[16,80,128]{2,1,0:T(8,128)}), f32[16,80,128]{2,1,0:T(8,128)S(1)}, u32[]{:S(2)}, u32[]{:S(2)}) async-start(f32[16,80,128]{2,1,0:T(8,128)} %get-tuple-element.27), calls=%async_computation | async-start | bytes 1310720 | tf_op jit(solution)/shard_map/all_to_all | solution.py:664
  69.2 0.0 copy-done
  69.2 0.1 copy.9
  69.3 1.7 %shard_map.79 = (bf16[256,768]{1,0:T(8,128)(2,1)S(1)}, f32[8,128]{1,0:T(8,128)S(1)}) custom-call(f32[256,256]{1,0:T(8,128)S(1)} %copy-done, f32[256,256]{1,0:T(8,128)S(1)} %bitcast.5), custom_call_target="tpu_custom_call" | custom-call | tf_op jit(solution)/shard_map/pallas_call | solution.py:676
  71.1 2.6 %shard_map.81 = (f32[5,256,128]{2,1,0:T(8,128)S(1)}, f32[5,256,128]{2,1,0:T(8,128)S(1)}) custom-call(f32[2,9]{1,0:T(2,128)S(1)} %copy-done.1, f32[16,80,128]{2,1,0:T(8,128)S(1)} %all-to-all-done.1.a_1_), custom_call_target="tpu_custom_call" | custom-call | tf_op jit(solution)/shard_map/pallas_call | solution.py:671
  73.7 12.0 %all-to-all-done.a_1_ = f32[16,80,128]{2,1,0:T(8,128)S(1)} async-done(((f32[16,80,128]{2,1,0:T(8,128)}), f32[16,80,128]{2,1,0:T(8,128)S(1)}, u32[]{:S(2)}, u32[]{:S(2)}) %all-to-all-start) | async-done | bytes 655392 | tf_op jit(solution)/shard_map/all_to_all | solution.py:664
  85.8 13.3 %shard_map.82 = (f32[4,5,256,128]{3,2,1,0:T(8,128)S(1)}, f32[32,128]{1,0:T(8,128)S(1)}) custom-call(f32[2,9]{1,0:T(2,128)S(1)} %copy-done.1, f32[16,80,128]{2,1,0:T(8,128)S(1)} %all-to-all-done.a_1_, bf16[256,768]{1,0:T(8,128)(2,1)S(1)} %get-tuple-element.28.a_2_, f32[8,128]{1,0:T(8,128)S(1)} %get-tuple-element.29.a_3_, ...), custom_call_target="tpu_custom_call" | custom-call | tf_op jit(solution)/shard_map/pallas_call | solution.py:690
  99.0 10.7 %all_to_all.20 = f32[32,1,128]{2,1,0:T(1,128)S(1)} all-to-all(f32[32,1,128]{2,1,0:T(1,128)S(1)} %bitcast.7), channel_id=1, replica_groups=mesh['gx'=16,'gy'=2] {'gx','gy'}, dimensions={0} | all-to-all | bytes 32768 | tf_op jit(solution)/shard_map/all_to_all | solution.py:698
  109.7 2.4 %shard_map.83 = f32[16,32,128]{2,1,0:T(8,128)S(1)} custom-call(f32[32,128]{1,0:T(8,128)S(1)} %bitcast.6, f32[4,5,256,128]{3,2,1,0:T(8,128)S(1)} %get-tuple-element.33.a_1_), custom_call_target="tpu_custom_call" | custom-call | tf_op jit(solution)/shard_map/pallas_call | solution.py:702
  112.2 12.6 %all_to_all.21.a_0_ = f32[16,32,128]{2,1,0:T(8,128)S(1)} all-to-all(f32[16,32,128]{2,1,0:T(8,128)S(1)} %shard_map.83), channel_id=1, replica_groups=mesh['gx'=16,'gy'=2] {'gx'}, dimensions={0} | all-to-all | bytes 524288 | tf_op jit(solution)/shard_map/all_to_all | solution.py:705
  124.8 1.8 %shard_map.84 = f32[16,32,128]{2,1,0:T(8,128)} custom-call(f32[16,32,128]{2,1,0:T(8,128)S(1)} %all_to_all.21.a_0_, f32[16,32,128]{2,1,0:T(8,128)S(1)} %get-tuple-element.19.a_2_.a_1_), custom_call_target="tpu_custom_call" | custom-call | tf_op jit(solution)/shard_map/pallas_call | solution.py:706
Async XLA Ops:
  0.6 38.3 %copy-start.1 = (f32[2,9]{1,0:T(2,128)S(1)}, f32[2,9]{1,0:T(2,128)}, u32[]{:S(2)}) copy-start(f32[2,9]{1,0:T(2,128)} %a_0_.7) | copy-start | bytes 220
  2.0 12.2 %collective-permute-start = (f32[3,16,16,128]{3,2,1,0:T(8,128)S(1)}, f32[3,16,16,128]{3,2,1,0:T(8,128)S(1)}, u32[]{:S(2)}, u32[]{:S(2)}) collective-permute-start(f32[3,16,16,128]{3,2,1,0:T(8,128)S(1)} %get-tuple-element.21), channel_id=1, source_target_pairs={{0,1},{1,0},{2,3},{3,2},{4,5},{5,4},{6,7},{7,6},{8,9},{9,8},{10,11... | collective-permute-start | bytes 1179656 | tf_op jit(solution)/shard_map/ppermute | solution.py:657
  16.5 52.7 %copy-start = (f32[256,256]{1,0:T(8,128)S(1)}, f32[256,256]{1,0:T(8,128)}, u32[]{:S(2)}) copy-start(f32[256,256]{1,0:T(8,128)} %line.1) | copy-start | bytes 786436
  16.5 38.3 %all-to-all-start.1 = ((f32[16,80,128]{2,1,0:T(8,128)}), f32[16,80,128]{2,1,0:T(8,128)S(1)}, u32[]{:S(2)}, u32[]{:S(2)}) async-start(f32[16,80,128]{2,1,0:T(8,128)} %shard_map.80), calls=%async_computation.1 | async-start | bytes 1310720 | tf_op jit(solution)/shard_map/all_to_all | solution.py:664
  22.7 16.2 %collective-permute-start.1 = (f32[3,9,32,128]{3,2,1,0:T(8,128)S(1)}, f32[3,9,32,128]{3,2,1,0:T(8,128)S(1)}, u32[]{:S(2)}, u32[]{:S(2)}) collective-permute-start(f32[3,9,32,128]{3,2,1,0:T(8,128)S(1)} %get-tuple-element.22), channel_id=1, source_target_pairs={{0,2},{1,3},{2,4},{3,5},{4,6},{5,7},{6,8},{7,9},{8,10},{9,11},{10,... | collective-permute-start | bytes 1327112 | tf_op jit(solution)/shard_map/ppermute | solution.py:657
  25.1 13.8 %collective-permute-start.3 = (f32[3,9,32,128]{3,2,1,0:T(8,128)S(1)}, f32[3,9,32,128]{3,2,1,0:T(8,128)S(1)}, u32[]{:S(2)}, u32[]{:S(2)}) collective-permute-start(f32[3,9,32,128]{3,2,1,0:T(8,128)S(1)} %get-tuple-element.24), channel_id=1, source_target_pairs={{2,0},{3,1},{4,2},{5,3},{6,4},{7,5},{8,6},{9,7},{10,8},{11,9},{12,... | collective-permute-start | bytes 1327112 | tf_op jit(solution)/shard_map/ppermute | solution.py:657
  26.4 8.7 %collective-permute-start.2 = (f32[3,9,16,128]{3,2,1,0:T(8,128)S(1)}, f32[3,9,16,128]{3,2,1,0:T(8,128)S(1)}, u32[]{:S(2)}, u32[]{:S(2)}) collective-permute-start(f32[3,9,16,128]{3,2,1,0:T(8,128)S(1)} %get-tuple-element.23), channel_id=1, source_target_pairs={{0,3},{1,2},{2,5},{3,4},{4,7},{5,6},{6,9},{7,8},{8,11},{9,10},{10,... | collective-permute-start | bytes 663560 | tf_op jit(solution)/shard_map/ppermute | solution.py:657
  31.7 7.3 %collective-permute-start.4 = (f32[3,9,16,128]{3,2,1,0:T(8,128)S(1)}, f32[3,9,16,128]{3,2,1,0:T(8,128)S(1)}, u32[]{:S(2)}, u32[]{:S(2)}) collective-permute-start(f32[3,9,16,128]{3,2,1,0:T(8,128)S(1)} %get-tuple-element.25), channel_id=1, source_target_pairs={{2,1},{3,0},{4,3},{5,2},{6,5},{7,4},{8,7},{9,6},{10,9},{11,8},{12,... | collective-permute-start | bytes 663560 | tf_op jit(solution)/shard_map/ppermute | solution.py:657
  54.7 31.0 %all-to-all-start = ((f32[16,80,128]{2,1,0:T(8,128)}), f32[16,80,128]{2,1,0:T(8,128)S(1)}, u32[]{:S(2)}, u32[]{:S(2)}) async-start(f32[16,80,128]{2,1,0:T(8,128)} %get-tuple-element.27), calls=%async_computation | async-start | bytes 1310720 | tf_op jit(solution)/shard_map/all_to_all | solution.py:664

commit v2 on v1

--- a/solution.py
+++ b/solution.py
@@ -9,7 +9,7 @@
 CHEB = 8
 ITERS = 4
 SUB = 8
-ROWS = 4
+TRIP = 48
 TILES = 8
 
 time_step = 2.0
@@ -18,7 +18,7 @@
 gain_top = 3.0625
 f32 = jnp.float32
 VMEM = pl.BlockSpec(memory_space=pltpu.VMEM)
-SMEM = pl.BlockSpec(memory_space=pltpu.SMEM)
+ANY = pl.BlockSpec(memory_space=pl.ANY)
 
 
 def up_to(n, m):
@@ -58,6 +58,14 @@
 
 def here():
     return lax.axis_index("gx"), lax.axis_index("gy")
+
+
+def block_rows(count, tiles):
+    def cost(r):
+        trips = -(-count // r)
+        return trips * (150 + 9 * r * tiles) if trips * r - count < SUB - 1 else 1 << 30
+
+    return min(range(1, max(2, TRIP // tiles + 1)), key=cost)
 
 
 def prep_kernel(plan, volt_hbm, pot_hbm, tissue_hbm, gain_hbm, volt, pot, cond, *rest):
@@ -117,14 +125,16 @@
     return same + (plus + minus)
 
 
-def cheb_kernel(plan, coup, volt, pot, cond, *rest):
+def cheb_kernel(plan, coup_any, volt, pot, cond, *rest):
     p = plan
     idx = here()
     ny_halo = 1 if p.swap else 2
     n_in = ny_halo + len(p.hops) * 2 * (1 + ny_halo)
     halos = rest[:n_in]
     new_volt, send = rest[n_in : n_in + 2]
-    C, G0, G1, E, PT, R, U, D, C2 = rest[n_in + 2 :]
+    C, G0, G1, E, PT, R, U, D, C2, coup, sem = rest[n_in + 2 :]
+    move = pltpu.make_async_copy(coup_any, coup, sem)
+    move.start()
     nx = p.nx
     flat = lambda ref: ref.reshape(p.yrows * p.zrows, nx)
     if p.swap:
@@ -186,6 +196,7 @@
 
     lane = lax.broadcasted_iota(jnp.int32, (SUB, nx), 1)
     left, right = lane == 0, lane == nx - 1
+    move.wait()
     ki = [coup[0, k] for k in range(9)]
     ke = [coup[1, k] for k in range(9)]
     total, ke_sum = ki[0], ke[0]
@@ -207,16 +218,18 @@
         y0 = p.pad + (idx[1] * over if p.swap else over)
         count = p.ny + (d + p.depth) * (1 if p.swap else 2)
 
+        step = block_rows(count, tiles)
+
         def block(i, carry):
             stores = []
-            for r in range(ROWS):
+            for r in range(step):
                 for t in range(tiles):
-                    stores += body(y0 + i * ROWS + r, p.hz - d + t * SUB)
+                    stores += body(y0 + i * step + r, p.hz - d + t * SUB)
             for ref, where, value in stores:
                 ref[where] = value
             return carry
 
-        lax.fori_loop(0, -(-count // ROWS), block, 0)
+        lax.fori_loop(0, -(-count // step), block, 0)
 
     def tile_of(ref, y, z):
         return lambda dz, dy: ref[y + dy, pl.ds(z + dz, SUB), :]
@@ -390,138 +403,154 @@
 
     def spread(self, recv, put):
         p = self.p
-        for s in range(p.slabs):
+
+        def one(s, carry):
             keep = self.inside(s)
             for j in range(p.ngx):
                 for zt in range(p.nz // SUB):
-                    got = recv[j, pl.ds(s * p.nz + zt * SUB, SUB), :]
+                    got = recv[j, pl.ds(pl.multiple_of(s * p.nz, SUB) + zt * SUB, SUB), :]
                     put(s, j * p.nz + zt * SUB, jnp.where(keep, got, 0.0))
+            return carry
+
+        lax.fori_loop(0, p.slabs, one, 0)
 
     def tile_of(self, ref, s, z):
         return lambda dz, dy: ref[s + 1 + dy, pl.ds(SUB + z + dz, SUB), :]
 
 
-def line_kernel(plan, coup, recv, C, CS, G):
+def line_kernel(plan, coup_any, recv, C, CS, G, coup, sem):
     p = plan
     nx = p.nx
+    move = pltpu.make_async_copy(coup_any, coup, sem)
+    move.start()
     geo = Line(p)
+    geo.edges(G)
+
+    def put(s, z, val):
+        C[s, pl.ds(z, SUB), :] = val
+        G[s + 1, pl.ds(SUB + z, SUB), :] = val
+
+    geo.spread(recv, put)
+    geo.wrap(G)
+    move.wait()
     ki = mixed([coup[0, k] for k in range(9)])
     ke_sum = coup[1, 0]
     for k in range(1, 9):
         ke_sum = ke_sum + coup[1, k]
     ke_twice = 2.0 * ke_sum
-    geo.edges(G)
-
-    def put(s, z, val):
-        C[s, pl.ds(z, SUB), :] = val
-        G[s + 1, pl.ds(SUB + z, SUB), :] = val
-
-    geo.spread(recv, put)
-    geo.wrap(G)
     step = TILES * SUB
-    for s in range(p.slabs):
-
-        def weigh(t, carry, s=s):
-            vals = []
-            for k in range(TILES):
-                z = pl.multiple_of(t * step, step) + k * SUB
+
+    def weigh(t, carry):
+        vals = []
+        for k in range(TILES):
+            z = pl.multiple_of(t * step, step) + k * SUB
+            for s in range(p.slabs):
                 part = combine(geo.tile_of(G, s, z), ki, None, None, nx)
-                vals.append((z, ke_twice + C[s, pl.ds(z, SUB), :] * part))
-            for z, v in vals:
-                CS[s, pl.ds(z, SUB), :] = v
-            return carry
-
-        lax.fori_loop(0, p.NZ // step, weigh, 0)
-
-
-def basis_kernel(plan, coup, recv, factor, size, C, CS, basis, sums, G, W, B0, B1, B2, R0, BB):
+                vals.append((s, z, ke_twice + C[s, pl.ds(z, SUB), :] * part))
+        for s, z, v in vals:
+            CS[s, pl.ds(z, SUB), :] = v
+        return carry
+
+    lax.fori_loop(0, p.NZ // step, weigh, 0)
+
+
+def basis_kernel(plan, coup_any, recv, factor, size, C, CS, basis, sums, G, W, B, R0, BB, keep, own, coup, sem):
     p = plan
-    nx, off = p.nx, SUB
+    nx, off, n = p.nx, SUB, p.depth
+    move = pltpu.make_async_copy(coup_any, coup, sem)
+    move.start()
     geo = Line(p)
-    wrap, tile_of, inside, own = geo.wrap, geo.tile_of, geo.inside, geo.own
-    ki = [coup[0, k] for k in range(9)]
-    ke = [coup[1, k] for k in range(9)]
-    ki_sum, ke_sum = ki[0], ke[0]
-    for k in range(1, 9):
-        ki_sum = ki_sum + ki[k]
-        ke_sum = ke_sum + ke[k]
-    lam = 2.0 * (ki_sum + ke_sum) * size[...]
-    quarter = 4.0 / lam
-    ki, ke = mixed(ki), mixed(ke)
     step = TILES * SUB
     geo.edges(G)
     geo.edges(W)
 
     def put(s, z, val):
-        B0[s, pl.ds(z, SUB), :] = val
-        R0[s, pl.ds(z, SUB), :] = val
+        rows = pl.ds(z, SUB)
+        B[0, s, rows, :] = val
+        R0[s, rows, :] = val
 
     geo.spread(recv, put)
-
-    ring = [B0, B1, B2]
-    out = jnp.zeros((1, nx), f32)
-
-    def lane_put(out, acc, at):
-        v = jnp.sum(jnp.sum(acc, axis=1, keepdims=True), axis=0, keepdims=True)
-        return jnp.where(lax.broadcasted_iota(jnp.int32, (1, nx), 1) == at, v, out)
-
+    move.wait()
+    ki = [coup[0, k] for k in range(9)]
+    ke = [coup[1, k] for k in range(9)]
+    total = ki[0] + ke[0]
+    for k in range(1, 9):
+        total = total + (ki[k] + ke[k])
+    quarter = 2.0 / (total * size[...])
+    ki, ke = mixed(ki), mixed(ke)
     zero = jnp.zeros((SUB, nx), f32)
-    slot = p.depth
-    for j in range(p.depth):
-        cur = ring[j % 3]
-        prev = ring[(j + 2) % 3]
-        new = ring[(j + 1) % 3]
-        for s in range(p.slabs):
-            b = cur[s]
+    lane_row = lax.broadcasted_iota(jnp.int32, (1, nx), 1)
+
+    def vectors(j):
+        cur = j % 3
+
+        def split(s, carry):
+            b = B[cur, s]
             high = b.astype(jnp.bfloat16)
-            cols = pl.ds(s * nx, nx)
+            cols = pl.ds(pl.multiple_of(s * nx, nx), nx)
             BB[pl.ds(0, p.NZ), cols] = high
             BB[pl.ds(p.NZ, p.NZ), cols] = high
             BB[pl.ds(2 * p.NZ, p.NZ), cols] = (b - high.astype(f32)).astype(jnp.bfloat16)
+            return carry
+
+        lax.fori_loop(0, p.slabs, split, 0)
         prod = jnp.dot(factor[...], BB[...], preferred_element_type=f32)
+        body = pl.ds(off, p.NZ)
         for s in range(p.slabs):
             part = prod[:, s * nx : (s + 1) * nx]
             basis[j, s] = part
-            W[s + 1, pl.ds(off, p.NZ), :] = part
-            G[s + 1, pl.ds(off, p.NZ), :] = part * C[s]
-        wrap(W)
-        wrap(G)
-        accs = [zero] * (j + 2)
-        for s in range(p.slabs):
-            keep = inside(s)
-
-            def apply(t, carry, s=s, keep=keep, j=j, cur=cur, prev=prev, new=new):
-                res = list(carry)
-                stores = []
-                for k in range(TILES):
-                    z = pl.multiple_of(t * step, step) + k * SUB
-                    rows = pl.ds(z, SUB)
+            W[s + 1, body, :] = part
+            G[s + 1, body, :] = part * C[s]
+        geo.wrap(W)
+        geo.wrap(G)
+
+    def apply(j):
+        cur, prev, new = j % 3, (j + 2) % 3, (j + 1) % 3
+        last = j == n - 1
+        gain_e = quarter if j else 0.5 * quarter
+
+        def block(t, carry):
+            accs = [list(c) for c in carry]
+            stores = []
+            for k in range(TILES):
+                z = pl.multiple_of(t * step, step) + k * SUB
+                rows = pl.ds(z, SUB)
+                for s in range(p.slabs):
                     w = W[s + 1, pl.ds(off + z, SUB), :]
-                    inner = combine(tile_of(G, s, z), ki, None, None, nx)
-                    outer = combine(tile_of(W, s, z), ke, None, None, nx)
+                    inner = combine(geo.tile_of(G, s, z), ki, None, None, nx)
+                    outer = combine(geo.tile_of(W, s, z), ke, None, None, nx)
                     e = CS[s, rows, :] * w - C[s, rows, :] * inner - outer
-                    e = jnp.where(keep, e, 0.0)
-                    if j < p.depth - 1:
-                        b = cur[s, rows, :]
-                        if j == 0:
-                            stores.append((rows, 0.5 * quarter * e - b))
-                        else:
-                            stores.append((rows, quarter * e - 2.0 * b - prev[s, rows, :]))
-                    for i in range(j):
-                        res[i] = res[i] + basis[i, s, rows, :] * e
-                    res[j] = res[j] + w * e
-                    res[j + 1] = res[j + 1] + w * R0[s, rows, :]
-                for rows, value in stores:
-                    new[s, rows, :] = value
-                return tuple(res)
-
-            got = lax.fori_loop(0, p.NZ // step, apply, tuple([zero] * (j + 2)))
-            mine = own(s)
-            accs = [a + jnp.where(mine, g, 0.0) for a, g in zip(accs, got)]
-        out = lane_put(out, accs[j + 1], j)
+                    e = e * keep[s]
+                    if j == 0:
+                        stores.append((s, rows, gain_e * e - B[cur, s, rows, :]))
+                    elif not last:
+                        stores.append((s, rows, gain_e * e - 2.0 * B[cur, s, rows, :] - B[prev, s, rows, :]))
+                    e = e * own[s]
+                    for i in range(j + 1):
+                        v = w if i == j else basis[i, s, rows, :]
+                        accs[i][k % 2] = accs[i][k % 2] + v * e
+                    accs[j + 1][k % 2] = accs[j + 1][k % 2] + (w * own[s]) * R0[s, rows, :]
+            for s, rows, value in stores:
+                B[new, s, rows, :] = value
+            return tuple(tuple(a) for a in accs)
+
+        accs = lax.fori_loop(0, p.NZ // step, block, tuple((zero, zero) for _ in range(j + 2)))
+        return [a + b for a, b in accs]
+
+    def fill(out, acc, at):
+        v = jnp.sum(jnp.sum(acc, axis=0, keepdims=True), axis=1, keepdims=True)
+        return jnp.where(lane_row == at, v, out)
+
+    for s in range(p.slabs):
+        keep[s] = jnp.where(geo.inside(s), 1.0, 0.0)
+        own[s] = jnp.where(geo.own(s), 1.0, 0.0)
+    out = jnp.zeros((1, nx), f32)
+    for j in range(n):
+        vectors(j)
+        accs = apply(j)
+        out = fill(out, accs[j + 1], j)
         for i in range(j + 1):
-            out = lane_put(out, accs[i], slot)
-            slot += 1
+            out = fill(out, accs[i], n + n * j + i)
     sums[...] = jnp.broadcast_to(out, sums.shape)
 
 
@@ -535,11 +564,9 @@
 
     rhs = [get(j) for j in range(n)]
     A = [[None] * n for _ in range(n)]
-    slot = n
     for j in range(n):
         for i in range(j + 1):
-            A[i][j] = A[j][i] = get(slot)
-            slot += 1
+            A[i][j] = A[j][i] = get(n + n * j + i)
     diag = [A[i][i] for i in range(n)]
     inv = [None] * n
     for k in range(n):
@@ -657,6 +684,8 @@
         halos.append(lax.ppermute(x, ("gx", "gy"), pairs(*r)))
 
     line = pltpu.VMEM((p.slabs, p.NZ, nx), f32)
+    flag = pltpu.VMEM((p.slabs, SUB, nx), f32)
+    table = [pltpu.SMEM(couplings.shape, f32), pltpu.SemaphoreType.DMA]
     wide = pltpu.VMEM((p.slabs + 2, p.NZ + 2 * SUB, nx), f32)
     half = pltpu.VMEM((3 * p.NZ, p.slabs * nx), jnp.bfloat16)
 
@@ -669,7 +698,10 @@
     )(cond, *sides)
     recv_c = swap_lines(send_c)
     line_c, line_cs = call(
-        lambda *a: line_kernel(p, *a), [SMEM, VMEM], [sds((p.slabs, p.NZ, nx), f32)] * 2, [wide]
+        lambda *a: line_kernel(p, *a),
+        [ANY, VMEM],
+        [sds((p.slabs, p.NZ, nx), f32)] * 2,
+        [wide] + table,
     )(couplings, recv_c)
 
     n_line = line_factor.shape[0]
@@ -680,18 +712,18 @@
     ext = pltpu.VMEM((p.yrows, p.zrows, nx), f32)
     new_voltage, send = call(
         lambda *a: cheb_kernel(p, *a),
-        [SMEM] + [VMEM] * (3 + len(halos)),
+        [ANY] + [VMEM] * (3 + len(halos)),
         [sds(voltage.shape, f32), sds((ngx, p.slabs * nz, nx), f32)],
-        [ext] * 9,
+        [ext] * 9 + table,
         mib=24,
     )(couplings, volt, pot, cond, *halos)
 
     recv = swap_lines(send)
     basis, sums = call(
         lambda *a: basis_kernel(p, *a),
-        [SMEM] + [VMEM] * 5,
+        [ANY] + [VMEM] * 5,
         [sds((p.depth, p.slabs, p.NZ, nx), f32), sds((ngx * ngy, nx), f32)],
-        [wide, wide, line, line, line, line, half],
+        [wide, wide, pltpu.VMEM((3, p.slabs, p.NZ, nx), f32), line, half, flag, flag] + table,
         mib=24,
     )(couplings, recv, parts, size, line_c, line_cs)
 

time: 127 us -> 121 us (0.953)
  Pallas kernels: 41.3 us -> 34.1 us
  waiting for transfers between devices: 27.1 us -> 28.5 us
    pallas_call x3, Pallas kernels: 31.7 us -> 24.5 us  [the longest x1 12 us: bidomain_step(): call(lambda *a: cheb_kernel(p, *a), [ANY] + [VMEM] * (3 + len(halos)), [s...]
    all_to_all x2, waiting for transfers between devices: 12 us -> 13.4 us  [swap_lines(): return lax.all_to_all(x, 'gx', split_axis=0, concat_axis=0, tiled=True)]
  transfers between devices with their start and end apart: 7 -> 7, of which waited for: 4 -> 4; matrix products, arithmetic and copies ran while one was open for 0% -> 0% of each run, Pallas kernels for 16% -> 12%
where the time goes in v2:
time: 121 us
  Pallas kernels  34.1 us (28%)
  starting transfers between devices  34 us (28%)
  waiting for transfers between devices  28.5 us (24%)
  blocking collectives  23.3 us (19%)
    all_to_all x2, starting transfers between devices, swap_lines(): return lax.all_to_all(x, 'gx', split_axis=0, concat_axis=0, tiled=True)  20.7 us
    ppermute x5, waiting for transfers between devices, bidomain_step(): halos.append(lax.ppermute(x, ('gx', 'gy'), pairs(*r)))  15.1 us
    all_to_all x2, waiting for transfers between devices, swap_lines(): return lax.all_to_all(x, 'gx', split_axis=0, concat_axis=0, tiled=True)  13.4 us
    ppermute x5, starting transfers between devices, bidomain_step(): halos.append(lax.ppermute(x, ('gx', 'gy'), pairs(*r)))  13.3 us
    all_to_all x1, blocking collectives, bidomain_step(): home = lax.all_to_all(back, 'gx', split_axis=0, concat_axis=0, tiled=True)  12.6 us
    pallas_call x1, Pallas kernels, bidomain_step(): call(lambda *a: cheb_kernel(p, *a), [ANY] + [VMEM] * (3 + len(halos)), [s...  12 us
    pallas_call x1, Pallas kernels, bidomain_step(): call(lambda *a: basis_kernel(p, *a), [ANY] + [VMEM] * 5, [sds((p.depth, p...  11.2 us
    all_to_all x1, blocking collectives, bidomain_step(): lax.all_to_all(sums.reshape(ngx * ngy, 1, nx), ('gx', 'gy'), split_axis=0...  10.7 us
  transfers between devices with their start and end apart: 7, of which 4 were waited for; matrix products, arithmetic and copies ran while one was open for 0% of the time, Pallas kernels for 12%

profile of v2, /device:TPU:0, one launch (start us, length us, event | category | flops | bytes accessed | tf_op | source)
XLA Modules:
  0.0 120.7 jit_solution(7035734599148669847)
XLA Ops:
  0.6 0.0 copy-start.1
  0.6 1.3 %shard_map.77 = (f32[16,32,128]{2,1,0:T(8,128)S(1)}, f32[16,32,128]{2,1,0:T(8,128)S(1)}, f32[16,32,128]{2,1,0:T(8,128)S(1)}, f32[3,16,16,128]{3,2,1,0:T(8,128)S(...) custom-call(f32[16,32,128]{2,1,0:T(8,128)} %a_0_.4, ...), custom_call_target="tpu_custom_call" | custom-call | tf_op jit(solution)/shard_map/pallas_call | solution.py:676
  2.0 3.1 %collective-permute-start = (f32[3,16,16,128]{3,2,1,0:T(8,128)S(1)}, f32[3,16,16,128]{3,2,1,0:T(8,128)S(1)}, u32[]{:S(2)}, u32[]{:S(2)}) collective-permute-start(f32[3,16,16,128]{3,2,1,0:T(8,128)S(1)} %get-tuple-element.21), channel_id=1, source_target_pairs={{0,1},{1,0},{2,3},{3,2},{4,5},{5,4},{6,7},{7,6},{8,9},{9,8},{10,11... | collective-permute-start | bytes 1179656 | tf_op jit(solution)/shard_map/ppermute | solution.py:684
  5.0 9.1 %collective-permute-done.a_4_.a_1_ = f32[3,16,16,128]{3,2,1,0:T(8,128)S(1)} collective-permute-done((f32[3,16,16,128]{3,2,1,0:T(8,128)S(1)}, f32[3,16,16,128]{3,2,1,0:T(8,128)S(1)}, u32[]{:S(2)}, u32[]{:S(2)}) %collective-permute-start) | collective-permute-done | bytes 393248 | tf_op jit(solution)/shard_map/ppermute | solution.py:684
  14.2 2.3 %shard_map.80 = f32[16,80,128]{2,1,0:T(8,128)} custom-call(f32[16,32,128]{2,1,0:T(8,128)S(1)} %get-tuple-element.20.a_3_.a_0_, f32[3,16,16,128]{3,2,1,0:T(8,128)S(1)} %collective-permute-done.a_4_.a_1_), custom_call_target="tpu_custom_call" | custom-call | tf_op jit(solution)/shard_map/pallas_call | solution.py:696
  16.5 0.0 copy-start
  16.5 6.3 %all-to-all-start.1 = ((f32[16,80,128]{2,1,0:T(8,128)}), f32[16,80,128]{2,1,0:T(8,128)S(1)}, u32[]{:S(2)}, u32[]{:S(2)}) async-start(f32[16,80,128]{2,1,0:T(8,128)} %shard_map.80), calls=%async_computation.1 | async-start | bytes 1310720 | tf_op jit(solution)/shard_map/all_to_all | solution.py:693
  22.7 2.3 %collective-permute-start.1 = (f32[3,9,32,128]{3,2,1,0:T(8,128)S(1)}, f32[3,9,32,128]{3,2,1,0:T(8,128)S(1)}, u32[]{:S(2)}, u32[]{:S(2)}) collective-permute-start(f32[3,9,32,128]{3,2,1,0:T(8,128)S(1)} %get-tuple-element.22), channel_id=1, source_target_pairs={{0,2},{1,3},{2,4},{3,5},{4,6},{5,7},{6,8},{7,9},{8,10},{9,11},{10,... | collective-permute-start | bytes 1327112 | tf_op jit(solution)/shard_map/ppermute | solution.py:684
  25.1 1.3 %collective-permute-start.3 = (f32[3,9,32,128]{3,2,1,0:T(8,128)S(1)}, f32[3,9,32,128]{3,2,1,0:T(8,128)S(1)}, u32[]{:S(2)}, u32[]{:S(2)}) collective-permute-start(f32[3,9,32,128]{3,2,1,0:T(8,128)S(1)} %get-tuple-element.24), channel_id=1, source_target_pairs={{2,0},{3,1},{4,2},{5,3},{6,4},{7,5},{8,6},{9,7},{10,8},{11,9},{12,... | collective-permute-start | bytes 1327112 | tf_op jit(solution)/shard_map/ppermute | solution.py:684
  26.4 5.3 %collective-permute-start.2 = (f32[3,9,16,128]{3,2,1,0:T(8,128)S(1)}, f32[3,9,16,128]{3,2,1,0:T(8,128)S(1)}, u32[]{:S(2)}, u32[]{:S(2)}) collective-permute-start(f32[3,9,16,128]{3,2,1,0:T(8,128)S(1)} %get-tuple-element.23), channel_id=1, source_target_pairs={{0,3},{1,2},{2,5},{3,4},{4,7},{5,6},{6,9},{7,8},{8,11},{9,10},{10,... | collective-permute-start | bytes 663560 | tf_op jit(solution)/shard_map/ppermute | solution.py:684
  31.7 1.3 %collective-permute-start.4 = (f32[3,9,16,128]{3,2,1,0:T(8,128)S(1)}, f32[3,9,16,128]{3,2,1,0:T(8,128)S(1)}, u32[]{:S(2)}, u32[]{:S(2)}) collective-permute-start(f32[3,9,16,128]{3,2,1,0:T(8,128)S(1)} %get-tuple-element.25), channel_id=1, source_target_pairs={{2,1},{3,0},{4,3},{5,2},{6,5},{7,4},{8,7},{9,6},{10,9},{11,8},{12,... | collective-permute-start | bytes 663560 | tf_op jit(solution)/shard_map/ppermute | solution.py:684
  33.0 2.1 %collective-permute-done.2.a_6_ = f32[3,9,16,128]{3,2,1,0:T(8,128)S(1)} collective-permute-done((f32[3,9,16,128]{3,2,1,0:T(8,128)S(1)}, f32[3,9,16,128]{3,2,1,0:T(8,128)S(1)}, u32[]{:S(2)}, u32[]{:S(2)}) %collective-permute-start.2) | collective-permute-done | bytes 221216 | tf_op jit(solution)/shard_map/ppermute | solution.py:684
  35.1 3.8 %collective-permute-done.4.a_8_ = f32[3,9,16,128]{3,2,1,0:T(8,128)S(1)} collective-permute-done((f32[3,9,16,128]{3,2,1,0:T(8,128)S(1)}, f32[3,9,16,128]{3,2,1,0:T(8,128)S(1)}, u32[]{:S(2)}, u32[]{:S(2)}) %collective-permute-start.4) | collective-permute-done | bytes 221216 | tf_op jit(solution)/shard_map/ppermute | solution.py:684
  38.9 0.0 collective-permute-done.1.a_5_
  38.9 0.0 collective-permute-done.3.a_7_
  38.9 0.0 copy-done.1
  38.9 12.0 %shard_map.78 = (f32[16,32,128]{2,1,0:T(8,128)}, f32[16,80,128]{2,1,0:T(8,128)}) custom-call(f32[2,9]{1,0:T(2,128)S(1)} %copy-done.1, f32[16,32,128]{2,1,0:T(8,128)S(1)} %get-tuple-element.18.a_1_, f32[16,32,128]{2,1,0:T(8,128)S(1)} %get-tuple-element.19.a_2_.a_1_, f32[16,32,128]{2,1,0:T(8,128)S(1)} %get-tuple-element.20.a_3_.a_0_, ...), custom_call_target="tpu_custom_call" | custom-call | tf_op jit(solution)/shard_map/pallas_call | solution.py:713
  50.9 0.0 all-to-all-done.1.a_1_
  51.0 14.5 %all-to-all-start = ((f32[16,80,128]{2,1,0:T(8,128)}), f32[16,80,128]{2,1,0:T(8,128)S(1)}, u32[]{:S(2)}, u32[]{:S(2)}) async-start(f32[16,80,128]{2,1,0:T(8,128)} %get-tuple-element.27), calls=%async_computation | async-start | bytes 1310720 | tf_op jit(solution)/shard_map/all_to_all | solution.py:693
  65.4 0.0 copy-done
  65.4 0.1 copy.9
  65.6 1.7 %shard_map.79 = (bf16[256,768]{1,0:T(8,128)(2,1)S(1)}, f32[8,128]{1,0:T(8,128)S(1)}) custom-call(f32[256,256]{1,0:T(8,128)S(1)} %copy-done, f32[256,256]{1,0:T(8,128)S(1)} %bitcast.5), custom_call_target="tpu_custom_call" | custom-call | tf_op jit(solution)/shard_map/pallas_call | solution.py:708
  67.3 1.3 %shard_map.81 = (f32[5,256,128]{2,1,0:T(8,128)S(1)}, f32[5,256,128]{2,1,0:T(8,128)S(1)}) custom-call(f32[2,9]{1,0:T(2,128)S(1)} %copy-done.1, f32[16,80,128]{2,1,0:T(8,128)S(1)} %all-to-all-done.1.a_1_), custom_call_target="tpu_custom_call" | custom-call | tf_op jit(solution)/shard_map/pallas_call | solution.py:700
  68.6 13.4 %all-to-all-done.a_1_ = f32[16,80,128]{2,1,0:T(8,128)S(1)} async-done(((f32[16,80,128]{2,1,0:T(8,128)}), f32[16,80,128]{2,1,0:T(8,128)S(1)}, u32[]{:S(2)}, u32[]{:S(2)}) %all-to-all-start) | async-done | bytes 655392 | tf_op jit(solution)/shard_map/all_to_all | solution.py:693
  82.0 11.2 %shard_map.82 = (f32[4,5,256,128]{3,2,1,0:T(8,128)S(1)}, f32[32,128]{1,0:T(8,128)S(1)}) custom-call(f32[2,9]{1,0:T(2,128)S(1)} %copy-done.1, f32[16,80,128]{2,1,0:T(8,128)S(1)} %all-to-all-done.a_1_, bf16[256,768]{1,0:T(8,128)(2,1)S(1)} %get-tuple-element.28.a_2_, f32[8,128]{1,0:T(8,128)S(1)} %get-tuple-element.29.a_3_, ...), custom_call_target="tpu_custom_call" | custom-call | tf_op jit(solution)/shard_map/pallas_call | solution.py:722
  93.2 10.7 %all_to_all.20 = f32[32,1,128]{2,1,0:T(1,128)S(1)} all-to-all(f32[32,1,128]{2,1,0:T(1,128)S(1)} %bitcast.7), channel_id=1, replica_groups=mesh['gx'=16,'gy'=2] {'gx','gy'}, dimensions={0} | all-to-all | bytes 32768 | tf_op jit(solution)/shard_map/all_to_all | solution.py:730
  103.9 2.4 %shard_map.83 = f32[16,32,128]{2,1,0:T(8,128)S(1)} custom-call(f32[32,128]{1,0:T(8,128)S(1)} %bitcast.6, f32[4,5,256,128]{3,2,1,0:T(8,128)S(1)} %get-tuple-element.33.a_1_), custom_call_target="tpu_custom_call" | custom-call | tf_op jit(solution)/shard_map/pallas_call | solution.py:734
  106.3 12.6 %all_to_all.21.a_0_ = f32[16,32,128]{2,1,0:T(8,128)S(1)} all-to-all(f32[16,32,128]{2,1,0:T(8,128)S(1)} %shard_map.83), channel_id=1, replica_groups=mesh['gx'=16,'gy'=2] {'gx'}, dimensions={0} | all-to-all | bytes 524288 | tf_op jit(solution)/shard_map/all_to_all | solution.py:737
  118.9 1.8 %shard_map.84 = f32[16,32,128]{2,1,0:T(8,128)} custom-call(f32[16,32,128]{2,1,0:T(8,128)S(1)} %all_to_all.21.a_0_, f32[16,32,128]{2,1,0:T(8,128)S(1)} %get-tuple-element.19.a_2_.a_1_), custom_call_target="tpu_custom_call" | custom-call | tf_op jit(solution)/shard_map/pallas_call | solution.py:738
Async XLA Ops:
  0.6 38.3 %copy-start.1 = (f32[2,9]{1,0:T(2,128)S(1)}, f32[2,9]{1,0:T(2,128)}, u32[]{:S(2)}) copy-start(f32[2,9]{1,0:T(2,128)} %a_0_.7) | copy-start | bytes 220
  2.0 12.2 %collective-permute-start = (f32[3,16,16,128]{3,2,1,0:T(8,128)S(1)}, f32[3,16,16,128]{3,2,1,0:T(8,128)S(1)}, u32[]{:S(2)}, u32[]{:S(2)}) collective-permute-start(f32[3,16,16,128]{3,2,1,0:T(8,128)S(1)} %get-tuple-element.21), channel_id=1, source_target_pairs={{0,1},{1,0},{2,3},{3,2},{4,5},{5,4},{6,7},{7,6},{8,9},{9,8},{10,11... | collective-permute-start | bytes 1179656 | tf_op jit(solution)/shard_map/ppermute | solution.py:684
  16.5 49.0 %copy-start = (f32[256,256]{1,0:T(8,128)S(1)}, f32[256,256]{1,0:T(8,128)}, u32[]{:S(2)}) copy-start(f32[256,256]{1,0:T(8,128)} %line.1) | copy-start | bytes 786436
  16.5 34.5 %all-to-all-start.1 = ((f32[16,80,128]{2,1,0:T(8,128)}), f32[16,80,128]{2,1,0:T(8,128)S(1)}, u32[]{:S(2)}, u32[]{:S(2)}) async-start(f32[16,80,128]{2,1,0:T(8,128)} %shard_map.80), calls=%async_computation.1 | async-start | bytes 1310720 | tf_op jit(solution)/shard_map/all_to_all | solution.py:693
  22.7 16.2 %collective-permute-start.1 = (f32[3,9,32,128]{3,2,1,0:T(8,128)S(1)}, f32[3,9,32,128]{3,2,1,0:T(8,128)S(1)}, u32[]{:S(2)}, u32[]{:S(2)}) collective-permute-start(f32[3,9,32,128]{3,2,1,0:T(8,128)S(1)} %get-tuple-element.22), channel_id=1, source_target_pairs={{0,2},{1,3},{2,4},{3,5},{4,6},{5,7},{6,8},{7,9},{8,10},{9,11},{10,... | collective-permute-start | bytes 1327112 | tf_op jit(solution)/shard_map/ppermute | solution.py:684
  25.1 13.8 %collective-permute-start.3 = (f32[3,9,32,128]{3,2,1,0:T(8,128)S(1)}, f32[3,9,32,128]{3,2,1,0:T(8,128)S(1)}, u32[]{:S(2)}, u32[]{:S(2)}) collective-permute-start(f32[3,9,32,128]{3,2,1,0:T(8,128)S(1)} %get-tuple-element.24), channel_id=1, source_target_pairs={{2,0},{3,1},{4,2},{5,3},{6,4},{7,5},{8,6},{9,7},{10,8},{11,9},{12,... | collective-permute-start | bytes 1327112 | tf_op jit(solution)/shard_map/ppermute | solution.py:684
  26.4 8.7 %collective-permute-start.2 = (f32[3,9,16,128]{3,2,1,0:T(8,128)S(1)}, f32[3,9,16,128]{3,2,1,0:T(8,128)S(1)}, u32[]{:S(2)}, u32[]{:S(2)}) collective-permute-start(f32[3,9,16,128]{3,2,1,0:T(8,128)S(1)} %get-tuple-element.23), channel_id=1, source_target_pairs={{0,3},{1,2},{2,5},{3,4},{4,7},{5,6},{6,9},{7,8},{8,11},{9,10},{10,... | collective-permute-start | bytes 663560 | tf_op jit(solution)/shard_map/ppermute | solution.py:684
  31.7 7.3 %collective-permute-start.4 = (f32[3,9,16,128]{3,2,1,0:T(8,128)S(1)}, f32[3,9,16,128]{3,2,1,0:T(8,128)S(1)}, u32[]{:S(2)}, u32[]{:S(2)}) collective-permute-start(f32[3,9,16,128]{3,2,1,0:T(8,128)S(1)} %get-tuple-element.25), channel_id=1, source_target_pairs={{2,1},{3,0},{4,3},{5,2},{6,5},{7,4},{8,7},{9,6},{10,9},{11,8},{12,... | collective-permute-start | bytes 663560 | tf_op jit(solution)/shard_map/ppermute | solution.py:684
  51.0 31.0 %all-to-all-start = ((f32[16,80,128]{2,1,0:T(8,128)}), f32[16,80,128]{2,1,0:T(8,128)S(1)}, u32[]{:S(2)}, u32[]{:S(2)}) async-start(f32[16,80,128]{2,1,0:T(8,128)} %get-tuple-element.27), calls=%async_computation | async-start | bytes 1310720 | tf_op jit(solution)/shard_map/all_to_all | solution.py:693

commit v3 on v2

--- a/solution.py
+++ b/solution.py
@@ -51,6 +51,7 @@
             self.wid *= 2
         self.hx = (self.wid - self.cols) // 2
         self.grp = self.nx // self.wid
+        self.inner = self.ny // self.grp
         self.slabs = -(-(self.ny + 2 * self.depth) // self.grp)
         self.back_grp = self.nx // self.cols
         self.back = self.ny // self.back_grp
@@ -312,30 +313,42 @@
         send[j, pl.ds(row, SUB), :] = acc
 
 
-def cond_kernel(plan, cond, *rest):
+def cond_kernel(plan, cond, send):
     p = plan
-    *sides, send = rest
+    flat = cond.reshape(p.nz * p.ny, p.nx)
+    for s in range(p.inner):
+        for zt in range(p.nz // SUB):
+            src = [flat[pl.ds(zt * SUB * p.ny + q * p.inner + s, SUB, stride=p.ny), :] for q in range(p.grp)]
+            windows(p, src, send, s * p.nz + zt * SUB)
+
+
+def edge_kernel(plan, recv, *outs):
+    p = plan
     idx = here()
-    flat = cond.reshape(p.nz * p.ny, p.nx)
-    flats = [ref.reshape(3 * p.nz * p.hy, p.nx) for ref in sides]
-
-    def row_of(y, zt):
-        if 0 <= y < p.ny:
-            return flat[pl.ds(zt * SUB * p.ny + y, SUB, stride=p.ny), :]
-        low = y < 0
-        at = p.hy + y if low else y - p.ny
-        if at >= p.hy:
-            return jnp.zeros((SUB, p.nx), f32)
-        ref = flats[0] if low else flats[-1]
-        val = ref[pl.ds((2 * p.nz + zt * SUB) * p.hy + at, SUB, stride=p.hy), :]
+    group = lax.broadcasted_iota(jnp.int32, (SUB, p.nx), 1) // p.wid
+    per = p.nz // SUB
+
+    def pick(t, y0):
+        acc = jnp.zeros((SUB, p.nx), f32)
+        for i in range(p.depth):
+            q, s = (y0 + i) // p.inner, (y0 + i) % p.inner
+            amount = (p.wid * (i - q)) % p.nx
+            part = recv[t // per, pl.ds(pl.multiple_of(s * p.nz + (t % per) * SUB, SUB), SUB), :]
+            part = pltpu.roll(part, amount, 1) if amount else part
+            acc = jnp.where(group == i, part, acc)
+        return acc
+
+    def one(t, carry):
+        rows = pl.ds(pl.multiple_of(t * SUB, SUB), SUB)
+        head, tail = pick(t, 0), pick(t, p.ny - p.depth)
         if p.swap:
-            val = jnp.where(idx[1] == (1 if low else 0), val, 0.0)
-        return val
-
-    for s in range(p.slabs):
-        for zt in range(p.nz // SUB):
-            src = [row_of(q * p.slabs + s - p.depth, zt) for q in range(p.grp)]
-            windows(p, src, send, s * p.nz + zt * SUB)
+            outs[0][rows, :] = jnp.where(idx[1] == 0, tail, head)
+        else:
+            outs[0][rows, :] = tail
+            outs[1][rows, :] = head
+        return carry
+
+    lax.fori_loop(0, p.NZ // SUB, one, 0, unroll=4)
 
 
 def factor_kernel(line, line_t, parts, size):
@@ -418,19 +431,47 @@
         return lambda dz, dy: ref[s + 1 + dy, pl.ds(SUB + z + dz, SUB), :]
 
 
-def line_kernel(plan, coup_any, recv, C, CS, G, coup, sem):
+def line_kernel(plan, coup_any, recv, *rest):
     p = plan
+    *edges, C, CS, G, coup, sem = rest
     nx = p.nx
     move = pltpu.make_async_copy(coup_any, coup, sem)
     move.start()
     geo = Line(p)
     geo.edges(G)
-
-    def put(s, z, val):
-        C[s, pl.ds(z, SUB), :] = val
-        G[s + 1, pl.ds(SUB + z, SUB), :] = val
-
-    geo.spread(recv, put)
+    group = geo.lane // p.wid
+    per = p.nz // SUB
+    masks = [geo.inside(s) for s in range(p.slabs)]
+
+    def arrange(t, carry):
+        z = pl.multiple_of(t * SUB, SUB)
+        src = [
+            recv[t // per, pl.ds(pl.multiple_of(s * p.nz + (t % per) * SUB, SUB), SUB), :] for s in range(p.inner)
+        ]
+        low, high = edges[0][pl.ds(z, SUB), :], edges[-1][pl.ds(z, SUB), :]
+        vals = []
+        for s in range(p.slabs):
+            acc = jnp.zeros((SUB, nx), f32)
+            for q in range(p.grp):
+                y = q * p.slabs + s - p.depth
+                if y < 0:
+                    part, at = low, y + p.depth
+                elif y < p.ny:
+                    part, at = src[y % p.inner], y // p.inner
+                elif y < p.ny + p.depth:
+                    part, at = high, y - p.ny
+                else:
+                    continue
+                amount = (p.wid * (q - at)) % nx
+                part = pltpu.roll(part, amount, 1) if amount else part
+                acc = jnp.where(group == q, part, acc)
+            vals.append(jnp.where(masks[s], acc, 0.0))
+        for s, val in enumerate(vals):
+            C[s, pl.ds(z, SUB), :] = val
+            G[s + 1, pl.ds(SUB + z, SUB), :] = val
+        return carry
+
+    lax.fori_loop(0, p.NZ // SUB, arrange, 0)
     geo.wrap(G)
     move.wait()
     ki = mixed([coup[0, k] for k in range(9)])
@@ -692,17 +733,16 @@
     def swap_lines(x):
         return lax.all_to_all(x, "gx", split_axis=0, concat_axis=0, tiled=True)
 
-    sides = halos[: len(ysends)]
-    (send_c,) = call(
-        lambda *a: cond_kernel(p, *a), [VMEM] * (1 + len(sides)), [sds((ngx, p.slabs * nz, nx), f32)]
-    )(cond, *sides)
+    (send_c,) = call(lambda *a: cond_kernel(p, *a), [VMEM], [sds((ngx, p.inner * nz, nx), f32)])(cond)
     recv_c = swap_lines(send_c)
+    edges = call(lambda *a: edge_kernel(p, *a), [VMEM], [sds((p.NZ, nx), f32)] * len(ysends))(recv_c)
+    edges = [lax.ppermute(x, ("gx", "gy"), pairs(0, dy)) for x, dy in zip(edges, ysends)]
     line_c, line_cs = call(
         lambda *a: line_kernel(p, *a),
-        [ANY, VMEM],
+        [ANY] + [VMEM] * (1 + len(edges)),
         [sds((p.slabs, p.NZ, nx), f32)] * 2,
         [wide] + table,
-    )(couplings, recv_c)
+    )(couplings, recv_c, *edges)
 
     n_line = line_factor.shape[0]
     parts, size = call(

time: 121 us -> 111 us (0.917)
  waiting for transfers between devices: 28.5 us -> 20.9 us
  starting transfers between devices: 34 us -> 27.3 us
  Pallas kernels: 34.1 us -> 37.3 us
    all_to_all x2, waiting for transfers between devices: 13.4 us -> 6.19 us  [swap_lines(): return lax.all_to_all(x, 'gx', split_axis=0, concat_axis=0, tiled=True)]
    all_to_all x2, starting transfers between devices: 20.7 us -> 15.2 us  [swap_lines(): return lax.all_to_all(x, 'gx', split_axis=0, concat_axis=0, tiled=True)]
    pallas_call x2 -> x3, Pallas kernels: 3.55 us -> 6.46 us  [the longest x1 3.56 us: bidomain_step(): call(lambda *a: line_kernel(p, *a), [ANY] + [VMEM] * (1 + len(edges)), [s...]
    ppermute x5, starting transfers between devices: 13.3 us -> 10.5 us  [bidomain_step(): halos.append(lax.ppermute(x, ('gx', 'gy'), pairs(*r)))]
    ppermute x5, waiting for transfers between devices: 15.1 us -> 12.3 us  [bidomain_step(): halos.append(lax.ppermute(x, ('gx', 'gy'), pairs(*r)))]
    ppermute x0 -> x1, waiting for transfers between devices: none -> 2.45 us  [bidomain_step(): lax.ppermute(x, ('gx', 'gy'), pairs(0, dy))]
    ppermute x0 -> x1, starting transfers between devices: none -> 1.54 us  [bidomain_step(): lax.ppermute(x, ('gx', 'gy'), pairs(0, dy))]
  transfers between devices with their start and end apart: 7 -> 8, of which waited for: 4 -> 4; matrix products, arithmetic and copies ran while one was open for 0% -> 0% of each run, Pallas kernels for 12% -> 17%
where the time goes in v3:
time: 111 us
  Pallas kernels  37.3 us (34%)
  starting transfers between devices  27.3 us (25%)
  blocking collectives  24.2 us (22%)
  waiting for transfers between devices  20.9 us (19%)
    all_to_all x2, starting transfers between devices, swap_lines(): return lax.all_to_all(x, 'gx', split_axis=0, concat_axis=0, tiled=True)  15.2 us
    all_to_all x1, blocking collectives, bidomain_step(): home = lax.all_to_all(back, 'gx', split_axis=0, concat_axis=0, tiled=True)  12.6 us
    ppermute x5, waiting for transfers between devices, bidomain_step(): halos.append(lax.ppermute(x, ('gx', 'gy'), pairs(*r)))  12.3 us
    pallas_call x1, Pallas kernels, bidomain_step(): call(lambda *a: cheb_kernel(p, *a), [ANY] + [VMEM] * (3 + len(halos)), [s...  12 us
    all_to_all x1, blocking collectives, bidomain_step(): lax.all_to_all(sums.reshape(ngx * ngy, 1, nx), ('gx', 'gy'), split_axis=0...  11.6 us
    pallas_call x1, Pallas kernels, bidomain_step(): call(lambda *a: basis_kernel(p, *a), [ANY] + [VMEM] * 5, [sds((p.depth, p...  11.5 us
    ppermute x5, starting transfers between devices, bidomain_step(): halos.append(lax.ppermute(x, ('gx', 'gy'), pairs(*r)))  10.5 us
    all_to_all x2, waiting for transfers between devices, swap_lines(): return lax.all_to_all(x, 'gx', split_axis=0, concat_axis=0, tiled=True)  6.19 us
  transfers between devices with their start and end apart: 8, of which 4 were waited for; matrix products, arithmetic and copies ran while one was open for 0% of the time, Pallas kernels for 17%

profile of v3, /device:TPU:0, one launch (start us, length us, event | category | flops | bytes accessed | tf_op | source)
XLA Modules:
  0.0 110.7 jit_solution(18403725097802520395)
XLA Ops:
  0.6 0.0 copy-start.1
  0.6 1.3 %shard_map.77 = (f32[16,32,128]{2,1,0:T(8,128)S(1)}, f32[16,32,128]{2,1,0:T(8,128)S(1)}, f32[16,32,128]{2,1,0:T(8,128)S(1)}, f32[3,16,16,128]{3,2,1,0:T(8,128)S(...) custom-call(f32[16,32,128]{2,1,0:T(8,128)} %a_0_.4, ...), custom_call_target="tpu_custom_call" | custom-call | tf_op jit(solution)/shard_map/pallas_call | solution.py:717
  2.0 2.0 %shard_map.80 = f32[16,64,128]{2,1,0:T(8,128)} custom-call(f32[16,32,128]{2,1,0:T(8,128)S(1)} %get-tuple-element.20.a_3_.a_0_), custom_call_target="tpu_custom_call" | custom-call | tf_op jit(solution)/shard_map/pallas_call | solution.py:736
  4.0 0.0 copy-start
  4.0 7.5 %all-to-all-start.1 = ((f32[16,64,128]{2,1,0:T(8,128)}), f32[16,64,128]{2,1,0:T(8,128)S(1)}, u32[]{:S(2)}, u32[]{:S(2)}) async-start(f32[16,64,128]{2,1,0:T(8,128)} %shard_map.80), calls=%async_computation.1 | async-start | bytes 1048576 | tf_op jit(solution)/shard_map/all_to_all | solution.py:734
  11.5 2.3 %collective-permute-start.1 = (f32[3,9,32,128]{3,2,1,0:T(8,128)S(1)}, f32[3,9,32,128]{3,2,1,0:T(8,128)S(1)}, u32[]{:S(2)}, u32[]{:S(2)}) collective-permute-start(f32[3,9,32,128]{3,2,1,0:T(8,128)S(1)} %get-tuple-element.22), channel_id=1, source_target_pairs={{0,2},{1,3},{2,4},{3,5},{4,6},{5,7},{6,8},{7,9},{8,10},{9,11},{10,... | collective-permute-start | bytes 1327112 | tf_op jit(solution)/shard_map/ppermute | solution.py:725
  13.8 1.3 %collective-permute-start.3 = (f32[3,9,32,128]{3,2,1,0:T(8,128)S(1)}, f32[3,9,32,128]{3,2,1,0:T(8,128)S(1)}, u32[]{:S(2)}, u32[]{:S(2)}) collective-permute-start(f32[3,9,32,128]{3,2,1,0:T(8,128)S(1)} %get-tuple-element.24), channel_id=1, source_target_pairs={{2,0},{3,1},{4,2},{5,3},{6,4},{7,5},{8,6},{9,7},{10,8},{11,9},{12,... | collective-permute-start | bytes 1327112 | tf_op jit(solution)/shard_map/ppermute | solution.py:725
  15.1 1.6 %collective-permute-start = (f32[3,16,16,128]{3,2,1,0:T(8,128)S(1)}, f32[3,16,16,128]{3,2,1,0:T(8,128)S(1)}, u32[]{:S(2)}, u32[]{:S(2)}) collective-permute-start(f32[3,16,16,128]{3,2,1,0:T(8,128)S(1)} %get-tuple-element.21), channel_id=1, source_target_pairs={{0,1},{1,0},{2,3},{3,2},{4,5},{5,4},{6,7},{7,6},{8,9},{9,8},{10,11... | collective-permute-start | bytes 1179656 | tf_op jit(solution)/shard_map/ppermute | solution.py:725
  16.7 4.0 %collective-permute-start.2 = (f32[3,9,16,128]{3,2,1,0:T(8,128)S(1)}, f32[3,9,16,128]{3,2,1,0:T(8,128)S(1)}, u32[]{:S(2)}, u32[]{:S(2)}) collective-permute-start(f32[3,9,16,128]{3,2,1,0:T(8,128)S(1)} %get-tuple-element.23), channel_id=1, source_target_pairs={{0,3},{1,2},{2,5},{3,4},{4,7},{5,6},{6,9},{7,8},{8,11},{9,10},{10,... | collective-permute-start | bytes 663560 | tf_op jit(solution)/shard_map/ppermute | solution.py:725
  20.7 1.3 %collective-permute-start.4 = (f32[3,9,16,128]{3,2,1,0:T(8,128)S(1)}, f32[3,9,16,128]{3,2,1,0:T(8,128)S(1)}, u32[]{:S(2)}, u32[]{:S(2)}) collective-permute-start(f32[3,9,16,128]{3,2,1,0:T(8,128)S(1)} %get-tuple-element.25), channel_id=1, source_target_pairs={{2,1},{3,0},{4,3},{5,2},{6,5},{7,4},{8,7},{9,6},{10,9},{11,8},{12,... | collective-permute-start | bytes 663560 | tf_op jit(solution)/shard_map/ppermute | solution.py:725
  22.0 10.1 %collective-permute-done.2.a_6_ = f32[3,9,16,128]{3,2,1,0:T(8,128)S(1)} collective-permute-done((f32[3,9,16,128]{3,2,1,0:T(8,128)S(1)}, f32[3,9,16,128]{3,2,1,0:T(8,128)S(1)}, u32[]{:S(2)}, u32[]{:S(2)}) %collective-permute-start.2) | collective-permute-done | bytes 221216 | tf_op jit(solution)/shard_map/ppermute | solution.py:725
  32.1 2.2 %collective-permute-done.4.a_8_ = f32[3,9,16,128]{3,2,1,0:T(8,128)S(1)} collective-permute-done((f32[3,9,16,128]{3,2,1,0:T(8,128)S(1)}, f32[3,9,16,128]{3,2,1,0:T(8,128)S(1)}, u32[]{:S(2)}, u32[]{:S(2)}) %collective-permute-start.4) | collective-permute-done | bytes 221216 | tf_op jit(solution)/shard_map/ppermute | solution.py:725
  34.3 0.0 collective-permute-done.a_4_
  34.3 0.0 collective-permute-done.1.a_5_
  34.3 0.0 collective-permute-done.3.a_7_
  34.3 0.0 copy-done.1
  34.3 12.0 %shard_map.78 = (f32[16,32,128]{2,1,0:T(8,128)}, f32[16,80,128]{2,1,0:T(8,128)}) custom-call(f32[2,9]{1,0:T(2,128)S(1)} %copy-done.1, f32[16,32,128]{2,1,0:T(8,128)S(1)} %get-tuple-element.18.a_1_, f32[16,32,128]{2,1,0:T(8,128)S(1)} %get-tuple-element.19.a_2_.a_1_, f32[16,32,128]{2,1,0:T(8,128)S(1)} %get-tuple-element.20.a_3_.a_0_, ...), custom_call_target="tpu_custom_call" | custom-call | tf_op jit(solution)/shard_map/pallas_call | solution.py:753
  46.4 0.0 all-to-all-done.1.a_0_.a_1_
  46.4 7.7 %all-to-all-start = ((f32[16,80,128]{2,1,0:T(8,128)}), f32[16,80,128]{2,1,0:T(8,128)S(1)}, u32[]{:S(2)}, u32[]{:S(2)}) async-start(f32[16,80,128]{2,1,0:T(8,128)} %get-tuple-element.27), calls=%async_computation | async-start | bytes 1310720 | tf_op jit(solution)/shard_map/all_to_all | solution.py:734
  54.1 0.9 shard_map.81
  55.1 1.5 %collective-permute-start.5 = (f32[256,128]{1,0:T(8,128)S(1)}, f32[256,128]{1,0:T(8,128)S(1)}, u32[]{:S(2)}, u32[]{:S(2)}) collective-permute-start(f32[256,128]{1,0:T(8,128)S(1)} %shard_map.81), channel_id=1, source_target_pairs={{0,1},{1,0},{2,3},{3,2},{4,5},{5,4},{6,7},{7,6},{8,9},{9,8},{10,11... | collective-permute-start | bytes 393224 | tf_op jit(solution)/shard_map/ppermute | solution.py:739
  56.6 0.0 copy-done
  56.6 0.1 copy.9
  56.7 1.7 %shard_map.79 = (bf16[256,768]{1,0:T(8,128)(2,1)S(1)}, f32[8,128]{1,0:T(8,128)S(1)}) custom-call(f32[256,256]{1,0:T(8,128)S(1)} %copy-done, f32[256,256]{1,0:T(8,128)S(1)} %bitcast.5), custom_call_target="tpu_custom_call" | custom-call | tf_op jit(solution)/shard_map/pallas_call | solution.py:748
  58.5 2.5 %collective-permute-done.5.a_2_ = f32[256,128]{1,0:T(8,128)S(1)} collective-permute-done((f32[256,128]{1,0:T(8,128)S(1)}, f32[256,128]{1,0:T(8,128)S(1)}, u32[]{:S(2)}, u32[]{:S(2)}) %collective-permute-start.5) | collective-permute-done | bytes 131104 | tf_op jit(solution)/shard_map/ppermute | solution.py:739
  60.9 3.6 %shard_map.82 = (f32[5,256,128]{2,1,0:T(8,128)S(1)}, f32[5,256,128]{2,1,0:T(8,128)S(1)}) custom-call(f32[2,9]{1,0:T(2,128)S(1)} %copy-done.1, f32[16,64,128]{2,1,0:T(8,128)S(1)} %all-to-all-done.1.a_0_.a_1_, f32[256,128]{1,0:T(8,128)S(1)} %collective-permute-done.5.a_2_), custom_call_target="tpu_custom_call" | custom-call | tf_op jit(solution)/shard_map/pallas_call | solution.py:740
  64.5 6.2 %all-to-all-done.a_1_ = f32[16,80,128]{2,1,0:T(8,128)S(1)} async-done(((f32[16,80,128]{2,1,0:T(8,128)}), f32[16,80,128]{2,1,0:T(8,128)S(1)}, u32[]{:S(2)}, u32[]{:S(2)}) %all-to-all-start) | async-done | bytes 655392 | tf_op jit(solution)/shard_map/all_to_all | solution.py:734
  70.7 11.5 %shard_map.83 = (f32[4,5,256,128]{3,2,1,0:T(8,128)S(1)}, f32[32,128]{1,0:T(8,128)S(1)}) custom-call(f32[2,9]{1,0:T(2,128)S(1)} %copy-done.1, f32[16,80,128]{2,1,0:T(8,128)S(1)} %all-to-all-done.a_1_, bf16[256,768]{1,0:T(8,128)(2,1)S(1)} %get-tuple-element.28.a_2_, f32[8,128]{1,0:T(8,128)S(1)} %get-tuple-element.29.a_3_, ...), custom_call_target="tpu_custom_call" | custom-call | tf_op jit(solution)/shard_map/pallas_call | solution.py:762
  82.2 11.6 %all_to_all.20 = f32[32,1,128]{2,1,0:T(1,128)S(1)} all-to-all(f32[32,1,128]{2,1,0:T(1,128)S(1)} %bitcast.7), channel_id=1, replica_groups=mesh['gx'=16,'gy'=2] {'gx','gy'}, dimensions={0} | all-to-all | bytes 32768 | tf_op jit(solution)/shard_map/all_to_all | solution.py:770
  93.8 2.4 %shard_map.84 = f32[16,32,128]{2,1,0:T(8,128)S(1)} custom-call(f32[32,128]{1,0:T(8,128)S(1)} %bitcast.6, f32[4,5,256,128]{3,2,1,0:T(8,128)S(1)} %get-tuple-element.33.a_1_), custom_call_target="tpu_custom_call" | custom-call | tf_op jit(solution)/shard_map/pallas_call | solution.py:774
  96.3 12.6 %all_to_all.21.a_0_ = f32[16,32,128]{2,1,0:T(8,128)S(1)} all-to-all(f32[16,32,128]{2,1,0:T(8,128)S(1)} %shard_map.84), channel_id=1, replica_groups=mesh['gx'=16,'gy'=2] {'gx'}, dimensions={0} | all-to-all | bytes 524288 | tf_op jit(solution)/shard_map/all_to_all | solution.py:777
  108.9 1.8 %shard_map.85 = f32[16,32,128]{2,1,0:T(8,128)} custom-call(f32[16,32,128]{2,1,0:T(8,128)S(1)} %all_to_all.21.a_0_, f32[16,32,128]{2,1,0:T(8,128)S(1)} %get-tuple-element.19.a_2_.a_1_), custom_call_target="tpu_custom_call" | custom-call | tf_op jit(solution)/shard_map/pallas_call | solution.py:778
Async XLA Ops:
  0.6 33.7 %copy-start.1 = (f32[2,9]{1,0:T(2,128)S(1)}, f32[2,9]{1,0:T(2,128)}, u32[]{:S(2)}) copy-start(f32[2,9]{1,0:T(2,128)} %a_0_.7) | copy-start | bytes 220
  4.0 52.6 %copy-start = (f32[256,256]{1,0:T(8,128)S(1)}, f32[256,256]{1,0:T(8,128)}, u32[]{:S(2)}) copy-start(f32[256,256]{1,0:T(8,128)} %line.1) | copy-start | bytes 786436
  4.0 42.4 %all-to-all-start.1 = ((f32[16,64,128]{2,1,0:T(8,128)}), f32[16,64,128]{2,1,0:T(8,128)S(1)}, u32[]{:S(2)}, u32[]{:S(2)}) async-start(f32[16,64,128]{2,1,0:T(8,128)} %shard_map.80), calls=%async_computation.1 | async-start | bytes 1048576 | tf_op jit(solution)/shard_map/all_to_all | solution.py:734
  11.5 22.8 %collective-permute-start.1 = (f32[3,9,32,128]{3,2,1,0:T(8,128)S(1)}, f32[3,9,32,128]{3,2,1,0:T(8,128)S(1)}, u32[]{:S(2)}, u32[]{:S(2)}) collective-permute-start(f32[3,9,32,128]{3,2,1,0:T(8,128)S(1)} %get-tuple-element.22), channel_id=1, source_target_pairs={{0,2},{1,3},{2,4},{3,5},{4,6},{5,7},{6,8},{7,9},{8,10},{9,11},{10,... | collective-permute-start | bytes 1327112 | tf_op jit(solution)/shard_map/ppermute | solution.py:725
  13.8 20.5 %collective-permute-start.3 = (f32[3,9,32,128]{3,2,1,0:T(8,128)S(1)}, f32[3,9,32,128]{3,2,1,0:T(8,128)S(1)}, u32[]{:S(2)}, u32[]{:S(2)}) collective-permute-start(f32[3,9,32,128]{3,2,1,0:T(8,128)S(1)} %get-tuple-element.24), channel_id=1, source_target_pairs={{2,0},{3,1},{4,2},{5,3},{6,4},{7,5},{8,6},{9,7},{10,8},{11,9},{12,... | collective-permute-start | bytes 1327112 | tf_op jit(solution)/shard_map/ppermute | solution.py:725
  15.1 19.2 %collective-permute-start = (f32[3,16,16,128]{3,2,1,0:T(8,128)S(1)}, f32[3,16,16,128]{3,2,1,0:T(8,128)S(1)}, u32[]{:S(2)}, u32[]{:S(2)}) collective-permute-start(f32[3,16,16,128]{3,2,1,0:T(8,128)S(1)} %get-tuple-element.21), channel_id=1, source_target_pairs={{0,1},{1,0},{2,3},{3,2},{4,5},{5,4},{6,7},{7,6},{8,9},{9,8},{10,11... | collective-permute-start | bytes 1179656 | tf_op jit(solution)/shard_map/ppermute | solution.py:725
  16.7 15.4 %collective-permute-start.2 = (f32[3,9,16,128]{3,2,1,0:T(8,128)S(1)}, f32[3,9,16,128]{3,2,1,0:T(8,128)S(1)}, u32[]{:S(2)}, u32[]{:S(2)}) collective-permute-start(f32[3,9,16,128]{3,2,1,0:T(8,128)S(1)} %get-tuple-element.23), channel_id=1, source_target_pairs={{0,3},{1,2},{2,5},{3,4},{4,7},{5,6},{6,9},{7,8},{8,11},{9,10},{10,... | collective-permute-start | bytes 663560 | tf_op jit(solution)/shard_map/ppermute | solution.py:725
  20.7 13.6 %collective-permute-start.4 = (f32[3,9,16,128]{3,2,1,0:T(8,128)S(1)}, f32[3,9,16,128]{3,2,1,0:T(8,128)S(1)}, u32[]{:S(2)}, u32[]{:S(2)}) collective-permute-start(f32[3,9,16,128]{3,2,1,0:T(8,128)S(1)} %get-tuple-element.25), channel_id=1, source_target_pairs={{2,1},{3,0},{4,3},{5,2},{6,5},{7,4},{8,7},{9,6},{10,9},{11,8},{12,... | collective-permute-start | bytes 663560 | tf_op jit(solution)/shard_map/ppermute | solution.py:725
  46.4 24.3 %all-to-all-start = ((f32[16,80,128]{2,1,0:T(8,128)}), f32[16,80,128]{2,1,0:T(8,128)S(1)}, u32[]{:S(2)}, u32[]{:S(2)}) async-start(f32[16,80,128]{2,1,0:T(8,128)} %get-tuple-element.27), calls=%async_computation | async-start | bytes 1310720 | tf_op jit(solution)/shard_map/all_to_all | solution.py:734
  55.1 5.9 %collective-permute-start.5 = (f32[256,128]{1,0:T(8,128)S(1)}, f32[256,128]{1,0:T(8,128)S(1)}, u32[]{:S(2)}, u32[]{:S(2)}) collective-permute-start(f32[256,128]{1,0:T(8,128)S(1)} %shard_map.81), channel_id=1, source_target_pairs={{0,1},{1,0},{2,3},{3,2},{4,5},{5,4},{6,7},{7,6},{8,9},{9,8},{10,11... | collective-permute-start | bytes 393224 | tf_op jit(solution)/shard_map/ppermute | solution.py:739
